TPU v7x, 32 devices: a whole 2x2x4 slice. The times are simulated.
32 devices in a mesh: rows: 16 (over z, x, core), cols: 2 (over y).
Axes of the slice: x: 2, y: 2, z: 4, core: 2. Of those that a mesh axis runs over, the one named last changes fastest.
Arguments:
- current_frame: bfloat16 [128, 256, 256], P(None, 'rows', 'cols'), may hold values from -6 to 6
- history_frames: bfloat16 [3, 128, 256, 256], P(None, None, 'rows', 'cols'), may hold values from -6 to 6
- offsets: int32 [3, 2], replicated, may hold values from -16 to 16, as said below
- compress_weight: bfloat16 [32, 128], replicated, may hold values from -0.5 to 0.5
- mixer_weight: bfloat16 [3, 3, 128, 224], replicated, may hold values from -0.125 to 0.125
- mixer_bias: float32 [128], replicated, may hold values from -3 to 3
Outputs:
- joined_grid: bfloat16 [128, 256, 256], P(None, 'rows', 'cols')
Inputs may be any that keep to these rules, and one draw needn't show every extreme that they name: offsets[k, 0] lies in -8..8 and offsets[k, 1] in -16..16; no offset is 0; in each of the two columns one frame's offset equals the bound and another equals its negative.
All inputs are finite; a program needn't handle non-finite values.
Results may differ from a plain program's by a relative error of at most 0.0034.
Values may be sent and summed in bfloat16 or wider, within the bound.
A program may use at most 64 MiB of HBM per device.

v0:
```python
import jax
import jax.numpy as jnp
from jax import lax
from jax.sharding import PartitionSpec as P

CP = 32
SHIFT_X = 16
SPLIT = True


def exchange(first, last, axis):
    size = lax.axis_size(axis)
    up = [(i, (i + 1) % size) for i in range(size - 1)]
    down = [(j, i) for i, j in up]
    return lax.ppermute(last, axis, up), lax.ppermute(first, axis, down)


def widen(block, rows, channels):
    return jnp.pad(block, ((0, rows - block.shape[0]), (0, 0), (0, channels - block.shape[2])))


def conv(block, weight):
    return lax.conv_general_dilated(
        block[None],
        weight,
        (1, 1),
        "VALID",
        dimension_numbers=("NHWC", "HWOI", "NHWC"),
        preferred_element_type=jnp.float32,
    )[0]


def body(current_frame, history_frames, offsets, compress_weight, mixer_weight, mixer_bias):
    frames, channels, height, width = history_frames.shape
    depth = frames * CP
    reach_rows = height // 2 + 1
    reach_cols = SHIFT_X + 1
    reduced = jnp.einsum(
        "oc,fcrx->rfox", compress_weight, history_frames, preferred_element_type=jnp.float32
    ).astype(jnp.bfloat16)
    source = reduced.reshape(height, depth, width).transpose(0, 2, 1)
    present = current_frame.transpose(1, 2, 0)
    wide = max(depth, channels)

    def row_pack(own, now):
        return jnp.concatenate([widen(own, reach_rows, wide), widen(now, 1, wide)], axis=0)

    above, below = exchange(
        row_pack(source[:reach_rows], present[:1]),
        row_pack(source[height - reach_rows :], present[height - 1 :]),
        "rows",
    )
    source = jnp.concatenate(
        [above[:reach_rows, :, :depth], source, below[:reach_rows, :, :depth]], axis=0
    )
    present = jnp.concatenate(
        [above[reach_rows:, :, :channels], present, below[reach_rows:, :, :channels]], axis=0
    )
    span = source.shape[0]

    def col_pack(own, now):
        return jnp.concatenate([widen(own, span, wide), widen(now, span, wide)], axis=1)

    left, right = exchange(
        col_pack(source[:, :reach_cols], present[:, :1]),
        col_pack(source[:, width - reach_cols :], present[:, width - 1 :]),
        "cols",
    )
    source = jnp.concatenate(
        [left[:, :reach_cols, :depth], source, right[:, :reach_cols, :depth]], axis=1
    )
    present = jnp.concatenate(
        [
            left[: height + 2, reach_cols:, :channels],
            present,
            right[: height + 2, reach_cols:, :channels],
        ],
        axis=1,
    )
    lane = lax.broadcasted_iota(jnp.int32, (1, 1, depth), 2) // CP
    shifted = None
    for k in range(frames):
        window = lax.dynamic_slice(
            source,
            (reach_rows - 1 - offsets[k, 0], reach_cols - 1 - offsets[k, 1], jnp.int32(0)),
            (height + 2, width + 2, depth),
        )
        shifted = window if shifted is None else jnp.where(lane == k, window, shifted)
    row = lax.broadcasted_iota(jnp.int32, (height + 2, 1, 1), 0) + (
        lax.axis_index("rows") * height - 1
    )
    col = lax.broadcasted_iota(jnp.int32, (1, width + 2, 1), 1) + (
        lax.axis_index("cols") * width - 1
    )
    inside = (row >= 0) & (row < height * lax.axis_size("rows"))
    inside = inside & (col >= 0) & (col < width * lax.axis_size("cols"))
    shifted = jnp.where(inside, shifted, jnp.zeros_like(shifted))
    if SPLIT:
        total = conv(present, mixer_weight[..., :channels])
        total = total + conv(shifted, mixer_weight[..., channels:])
    else:
        total = conv(jnp.concatenate([present, shifted], axis=2), mixer_weight)
    result = jnp.maximum(total + mixer_bias, 0.0).astype(jnp.bfloat16)
    return result.transpose(2, 0, 1)


def solution(mesh):
    in_specs = (P(None, "rows", "cols"), P(None, None, "rows", "cols"), P(), P(), P(), P())
    out_specs = P(None, "rows", "cols")
    return jax.shard_map(body, mesh=mesh, in_specs=in_specs, out_specs=out_specs, check_vma=False)
```

profile of v0, /device:TPU:1, one launch (start us, length us, event | category | flops | bytes accessed | tf_op | source)
XLA Modules:
  0.0 65.3 jit_solution(17658822021721244742)
XLA Ops:
  0.0 1.4 %copy-done = bf16[3,128,16,128]{3,2,1,0:T(8,128)(2,1)S(1)} copy-done((bf16[3,128,16,128]{3,2,1,0:T(8,128)(2,1)S(1)}, bf16[3,128,16,128]{3,2,1,0:T(8,128)(2,1)}, u32[]{:S(2)}) %copy-start) | copy-done | bytes 1572888
  1.4 1.1 %fusion.8 = bf16[16,3,32,128]{3,2,0,1:T(8,128)(2,1)S(1)} fusion(bf16[3,128,16,128]{3,2,1,0:T(8,128)(2,1)S(1)} %copy-done, bf16[32,128]{1,0:T(8,128)(2,1)} %param.9), kind=kOutput, calls=%fused_computation.11 | convolution fusion | flops 50528256 | bytes 1974272 | tf_op jit(solution)/shard_map/oc,fcrx->rfox/dot_general | solution.py:38
  2.8 1.9 %collective-permute-start.1 = (bf16[10,128,128]{1,2,0:T(8,128)(2,1)S(1)}, bf16[10,128,128]{1,2,0:T(8,128)(2,1)S(1)}, u32[]{:S(2)}, u32[]{:S(2)}) collective-permute-start(bf16[10,128,128]{1,2,0:T(8,128)(2,1)S(1)} %fusion.36), channel_id=1, source_target_pairs={{2,0},{4,2},{6,4},{8,6},{10,8},{12,10},{14,12},{16,14},{18,16},{20... | collective-permute-start | bytes 983048 | tf_op jit(solution)/shard_map/ppermute | solution.py:15
  4.7 4.5 %collective-permute-start = (bf16[10,128,128]{1,2,0:T(8,128)(2,1)S(1)}, bf16[10,128,128]{1,2,0:T(8,128)(2,1)}, u32[]{:S(2)}, u32[]{:S(2)}) collective-permute-start(bf16[10,128,128]{1,2,0:T(8,128)(2,1)S(1)} %fusion.35), channel_id=1, source_target_pairs={{0,2},{2,4},{4,6},{6,8},{8,10},{10,12},{12,14},{14,16},{16,18},{18... | collective-permute-start | bytes 983048 | tf_op jit(solution)/shard_map/ppermute | solution.py:15
  9.3 2.7 %collective-permute-done.1 = bf16[10,128,128]{1,2,0:T(8,128)(2,1)S(1)} collective-permute-done((bf16[10,128,128]{1,2,0:T(8,128)(2,1)S(1)}, bf16[10,128,128]{1,2,0:T(8,128)(2,1)S(1)}, u32[]{:S(2)}, u32[]{:S(2)}) %collective-permute-start.1) | collective-permute-done | bytes 327712 | tf_op jit(solution)/shard_map/ppermute | solution.py:15
  12.0 3.7 %collective-permute-done = bf16[10,128,128]{1,2,0:T(8,128)(2,1)} collective-permute-done((bf16[10,128,128]{1,2,0:T(8,128)(2,1)S(1)}, bf16[10,128,128]{1,2,0:T(8,128)(2,1)}, u32[]{:S(2)}, u32[]{:S(2)}) %collective-permute-start) | collective-permute-done | bytes 327712 | tf_op jit(solution)/shard_map/ppermute | solution.py:15
  15.7 0.8 %slice.106 = bf16[1,128,128]{1,2,0:T(8,128)(2,1)S(1)} slice(bf16[10,128,128]{1,2,0:T(8,128)(2,1)} %collective-permute-done), slice={[9:10], [0:128], [0:128]} | slice | bytes 65536 | tf_op jit(solution)/shard_map/slice | solution.py:57
  17.1 1.1 %fusion.51 = (bf16[18,1,128]{1,2,0:T(8,128)(2,1)}, bf16[18,1,128]{1,2,0:T(8,128)(2,1)S(1)}) fusion(bf16[18,128,128]{1,2,0:T(8,128)(2,1)S(1)} %pad_maximum_fusion.2), kind=kLoop, calls=%fused_computation.68 | loop fusion | bytes 18432 | tf_op jit(solution)/shard_map/slice | solution.py:66
  18.2 1.4 %copy.46 = bf16[18,1,128]{2,0,1:T(8,128)(2,1)S(1)} copy(bf16[18,1,128]{1,2,0:T(8,128)(2,1)} %get-tuple-element.7) | data formatting | bytes 9216
  19.6 0.9 %copy.48 = bf16[18,1,128]{2,0,1:T(8,128)(2,1)} copy(bf16[18,1,128]{1,2,0:T(8,128)(2,1)S(1)} %get-tuple-element.8) | data formatting | bytes 9216
  20.5 1.0 %slice.101 = bf16[9,128,96]{1,2,0:T(8,128)(2,1)S(1)} slice(bf16[10,128,128]{1,2,0:T(8,128)(2,1)} %collective-permute-done), slice={[0:9], [0:128], [0:96]} | slice | bytes 442368 | tf_op jit(solution)/shard_map/slice | solution.py:54
  22.4 1.2 %fusion.50 = (bf16[34,17,96]{1,2,0:T(8,128)(2,1)}, bf16[34,17,96]{1,2,0:T(8,128)(2,1)S(1)}) fusion(bf16[34,128,96]{1,2,0:T(8,128)(2,1)S(1)} %pad_maximum_fusion.1), kind=kLoop, calls=%fused_computation.67 | loop fusion | bytes 443904 | tf_op jit(solution)/shard_map/slice | solution.py:66
  23.6 1.6 %copy.45 = bf16[34,17,96]{2,0,1:T(8,128)(2,1)S(1)} copy(bf16[34,17,96]{1,2,0:T(8,128)(2,1)} %get-tuple-element.5) | data formatting | bytes 221952
  25.2 1.1 %copy.47 = bf16[34,17,96]{2,0,1:T(8,128)(2,1)} copy(bf16[34,17,96]{1,2,0:T(8,128)(2,1)S(1)} %get-tuple-element.6) | data formatting | bytes 221952
  26.3 1.0 %fusion.40 = bf16[34,18,128]{2,0,1:T(8,128)(2,1)S(1)} fusion(bf16[18,1,128]{2,0,1:T(8,128)(2,1)} %copy.48, bf16[34,17,96]{2,0,1:T(8,128)(2,1)} %copy.47), kind=kLoop, calls=%fused_computation.48 | loop fusion | flops 626688 | bytes 272256 | tf_op jit(solution)/shard_map/concatenate | solution.py:62
  27.2 1.3 %collective-permute-start.3 = (bf16[34,18,128]{2,0,1:T(8,128)(2,1)S(1)}, bf16[34,18,128]{2,0,1:T(8,128)(2,1)}, u32[]{:S(2)}, u32[]{:S(2)}) collective-permute-start(bf16[34,18,128]{2,0,1:T(8,128)(2,1)S(1)} %fusion.40), channel_id=1, source_target_pairs={{1,0},{3,2},{5,4},{7,6},{9,8},{11,10},{13,12},{15,14},{17,16},{19,... | collective-permute-start | bytes 470024 | tf_op jit(solution)/shard_map/ppermute | solution.py:15
  28.6 4.9 %collective-permute-start.2 = (bf16[34,18,128]{2,0,1:T(8,128)(2,1)S(1)}, bf16[34,18,128]{2,0,1:T(8,128)(2,1)S(1)}, u32[]{:S(2)}, u32[]{:S(2)}) collective-permute-start(bf16[34,18,128]{2,0,1:T(8,128)(2,1)S(1)} %fusion.39), channel_id=1, source_target_pairs={{0,1},{2,3},{4,5},{6,7},{8,9},{10,11},{12,13},{14,15},{16,17},{18,... | collective-permute-start | bytes 470024 | tf_op jit(solution)/shard_map/ppermute | solution.py:15
  41.8 0.7 %slice.112 = bf16[18,1,128]{2,0,1:T(8,128)(2,1)S(1)} slice(bf16[34,18,128]{2,0,1:T(8,128)(2,1)} %collective-permute-done.3), slice={[0:18], [17:18], [0:128]} | slice | bytes 9216 | tf_op jit(solution)/shard_map/slice | solution.py:76
  42.5 1.1 %copy.29 = bf16[18,1,128]{1,2,0:T(8,128)(2,1)} copy(bf16[18,1,128]{2,0,1:T(8,128)(2,1)S(1)} %slice.112) | data formatting | bytes 9216 | tf_op jit(solution)/shard_map/slice | solution.py:76
  43.6 2.8 %maximum_bitcast_fusion = bf16[18,1,130,128]{2,3,0,1:T(8,128)(2,1)} fusion(bf16[18,1,128]{1,2,0:T(8,128)(2,1)} %copy.29, bf16[1,128,128]{1,2,0:T(8,128)(2,1)S(1)} %slice.107, bf16[16,128,128]{1,2,0:T(8,128)(2,1)S(1)} %bitcast.61, bf16[1,128,128]{1,2,0:T(8,128)(2,1)S(1)} %copy-done.9, bf16[18,1,128]{1,2,0:T(8,128)(2,1)S(1)} %copy.28), kind=kLoop, calls=%fused_computation.12 | loop fusion | flops 2995200 | bytes 1198080 | tf_op jit(solution)/shard_map/broadcast_in_dim | solution.py:24
  46.4 1.7 %copy.49 = bf16[18,1,130,128]{3,2,0,1:T(8,128)(2,1)S(1)} copy(bf16[18,1,130,128]{2,3,0,1:T(8,128)(2,1)} %maximum_bitcast_fusion) | data formatting | bytes 1198080
  48.1 0.9 %pad.27.clone = bf16[18,1,136,128]{3,2,0,1:T(8,128)(2,1)} pad(bf16[18,1,130,128]{3,2,0,1:T(8,128)(2,1)S(1)} %copy.49, bf16[]{:T(256)} %constant.57.clone.1), padding=0_0x0_0x0_6x0_0 | pad | bytes 1225730 | tf_op jit(solution)/shard_map/broadcast_in_dim | solution.py:24
  49.0 1.3 %reshape.143 = bf16[18,1,8,17,128]{4,3,2,0,1:T(8,128)(2,1)S(1)} reshape(bf16[18,1,136,128]{3,2,0,1:T(8,128)(2,1)} %pad.27.clone) | data formatting | bytes 1253376 | tf_op jit(solution)/shard_map/conv_general_dilated | solution.py:23
  51.7 0.9 %slice.115 = bf16[34,17,96]{2,0,1:T(8,128)(2,1)S(1)} slice(bf16[34,18,128]{2,0,1:T(8,128)(2,1)} %collective-permute-done.3), slice={[0:34], [0:17], [0:96]} | slice | bytes 221952 | tf_op jit(solution)/shard_map/slice | solution.py:70
  52.7 1.3 %copy.44 = bf16[34,17,96]{1,2,0:T(8,128)(2,1)} copy(bf16[34,17,96]{2,0,1:T(8,128)(2,1)S(1)} %slice.115) | data formatting | bytes 221952
  54.0 2.1 %pad_maximum_fusion = bf16[34,162,96]{1,2,0:T(8,128)(2,1)S(1)} fusion(bf16[34,17,96]{1,2,0:T(8,128)(2,1)} %copy.44, bf16[9,128,96]{1,2,0:T(8,128)(2,1)S(1)} %copy-done.2, bf16[16,128,96]{1,2,0:T(8,128)(2,1)S(1)} %bitcast.58, bf16[9,128,96]{1,2,0:T(8,128)(2,1)S(1)} %copy-done.4, bf16[34,17,96]{1,2,0:T(8,128)(2,1)S(1)} %copy.43), kind=kLoop, calls=%fused_computation | loop fusion | flops 5287680 | bytes 2115072 | tf_op jit(solution)/shard_map/concatenate | solution.py:69
  56.1 1.2 %select_bitcast_fusion = bf16[18,1,130,96]{2,3,0,1:T(8,128)(2,1)S(1)} fusion(bf16[34,162,96]{1,2,0:T(8,128)(2,1)S(1)} %pad_maximum_fusion, s32[]{:T(128)S(6)} %select_n.49, s32[]{:T(128)S(6)} %select_n.50, s32[]{:T(128)S(6)} %select_n.47, s32[]{:T(128)S(6)} %select_n.48, s32[]{:T(128)S(6)} %select_n.45, s32[]{:T(128)S(6)} %select_n.46, ...), kind=kLoop, calls=%fused_computation.17 | loop fusion | flops 673920 | bytes 1799676 | tf_op jit(solution)/shard_map/broadcast_in_dim | solution.py:24
  57.8 1.0 %pad.29.clone = bf16[18,1,136,96]{3,2,0,1:T(8,128)(2,1)} pad(bf16[18,1,130,96]{3,2,0,1:T(8,128)(2,1)S(1)} %copy.50, bf16[]{:T(256)} %constant.57.clone.1), padding=0_0x0_0x0_6x0_0 | pad | bytes 919298 | tf_op jit(solution)/shard_map/broadcast_in_dim | solution.py:24
  58.7 1.4 %reshape.148 = bf16[18,1,8,17,96]{4,3,2,0,1:T(8,128)(2,1)S(1)} reshape(bf16[18,1,136,96]{3,2,0,1:T(8,128)(2,1)} %pad.29.clone) | data formatting | bytes 940032 | tf_op jit(solution)/shard_map/conv_general_dilated | solution.py:23
  60.3 1.2 %convolution_select_fusion = f32[16,8,17,128]{3,1,2,0:T(8,128)S(1)} fusion(bf16[18,1,7,2,96]{4,2,3,0,1:T(8,128)(2,1)S(1)} %slice.116, bf16[18,1,8,17,96]{4,2,3,0,1:T(8,128)(2,1)S(1)} %copy.38, pred[8,17]{0,1:T(8,128)(4,1)S(1)} %copy-done.16, bf16[3,3,128,224]{2,3,1,0:T(8,128)(2,1)S(1)} %copy-done.15), kind=kOutput, calls=%fused_computation.7 | convolution fusion | flops 483150848 | bytes 2038784 | tf_op jit(solution)/shard_map/conv_general_dilated | solution.py:23
  61.6 1.5 %fusion.4 = f32[16,8,17,128]{3,1,2,0:T(8,128)S(1)} fusion(f32[16,8,17,128]{3,1,2,0:T(8,128)S(1)} %convolution_select_fusion, bf16[18,1,7,2,128]{4,2,3,0,1:T(8,128)(2,1)S(1)} %copy-done.12, bf16[18,1,8,17,128]{4,2,3,0,1:T(8,128)(2,1)S(1)} %copy-done.6, pred[8,17]{0,1:T(8,128)(4,1)S(1)} %copy-done.16, bf16[3,3,128,224]{2,3,1,0:T(8,128)(2,1)S(1)} %copy-done.15), kind=kOutput, calls=%fused_computation.9 | convolution fusion | flops 644386816 | bytes 3226624 | tf_op jit(solution)/shard_map/conv_general_dilated | solution.py:23
  63.8 1.5 %copy.40 = bf16[128,16,128]{2,1,0:T(8,128)(2,1)} copy(bf16[128,16,128]{0,1,2:T(8,128)(2,1)S(1)} %fusion.28) | data formatting | bytes 1048576 | tf_op jit(solution)/shard_map/transpose | solution.py:104
  (62 shorter events, 5.6 us)
Async XLA Ops:
  0.0 1.4 %copy-start = (bf16[3,128,16,128]{3,2,1,0:T(8,128)(2,1)S(1)}, bf16[3,128,16,128]{3,2,1,0:T(8,128)(2,1)}, u32[]{:S(2)}) copy-start(bf16[3,128,16,128]{3,2,1,0:T(8,128)(2,1)} %param.7) | copy-start | bytes 4718596
  0.0 2.6 %copy-start.7 = (bf16[128,16,128]{2,1,0:T(8,128)(2,1)S(1)}, bf16[128,16,128]{2,1,0:T(8,128)(2,1)}, u32[]{:S(2)}) copy-start(bf16[128,16,128]{2,1,0:T(8,128)(2,1)} %param.6) | copy-start | bytes 1572868
  2.8 9.2 %collective-permute-start.1 = (bf16[10,128,128]{1,2,0:T(8,128)(2,1)S(1)}, bf16[10,128,128]{1,2,0:T(8,128)(2,1)S(1)}, u32[]{:S(2)}, u32[]{:S(2)}) collective-permute-start(bf16[10,128,128]{1,2,0:T(8,128)(2,1)S(1)} %fusion.36), channel_id=1, source_target_pairs={{2,0},{4,2},{6,4},{8,6},{10,8},{12,10},{14,12},{16,14},{18,16},{20... | collective-permute-start | bytes 983048 | tf_op jit(solution)/shard_map/ppermute | solution.py:15
  4.7 11.0 %collective-permute-start = (bf16[10,128,128]{1,2,0:T(8,128)(2,1)S(1)}, bf16[10,128,128]{1,2,0:T(8,128)(2,1)}, u32[]{:S(2)}, u32[]{:S(2)}) collective-permute-start(bf16[10,128,128]{1,2,0:T(8,128)(2,1)S(1)} %fusion.35), channel_id=1, source_target_pairs={{0,2},{2,4},{4,6},{6,8},{8,10},{10,12},{12,14},{14,16},{16,18},{18... | collective-permute-start | bytes 983048 | tf_op jit(solution)/shard_map/ppermute | solution.py:15
  16.4 0.6 copy-start.8
  20.5 1.1 %copy-start.1 = (bf16[9,128,96]{1,2,0:T(8,128)(2,1)}, bf16[9,128,96]{1,2,0:T(8,128)(2,1)S(1)}, u32[]{:S(2)}) copy-start(bf16[9,128,96]{1,2,0:T(8,128)(2,1)S(1)} %slice.104) | copy-start | bytes 663556
  21.6 0.7 %copy-start.3 = (bf16[9,128,96]{1,2,0:T(8,128)(2,1)}, bf16[9,128,96]{1,2,0:T(8,128)(2,1)S(1)}, u32[]{:S(2)}) copy-start(bf16[9,128,96]{1,2,0:T(8,128)(2,1)S(1)} %slice.101) | copy-start | bytes 663556
  23.6 9.8 %copy-start.13 = (s32[3,2]{0,1:T(2,128)S(1)}, s32[3,2]{0,1:T(2,128)}, u32[]{:S(2)}) copy-start(s32[3,2]{0,1:T(2,128)} %param.8) | copy-start | bytes 76
  26.3 17.3 %copy-start.9 = (bf16[1,128,128]{1,2,0:T(8,128)(2,1)S(1)}, bf16[1,128,128]{1,2,0:T(8,128)(2,1)}, u32[]{:S(2)}) copy-start(bf16[1,128,128]{1,2,0:T(8,128)(2,1)} %copy-done.8) | copy-start | bytes 98308
  27.2 14.6 %collective-permute-start.3 = (bf16[34,18,128]{2,0,1:T(8,128)(2,1)S(1)}, bf16[34,18,128]{2,0,1:T(8,128)(2,1)}, u32[]{:S(2)}, u32[]{:S(2)}) collective-permute-start(bf16[34,18,128]{2,0,1:T(8,128)(2,1)S(1)} %fusion.40), channel_id=1, source_target_pairs={{1,0},{3,2},{5,4},{7,6},{9,8},{11,10},{13,12},{15,14},{17,16},{19,... | collective-permute-start | bytes 470024 | tf_op jit(solution)/shard_map/ppermute | solution.py:15
  28.6 12.8 %collective-permute-start.2 = (bf16[34,18,128]{2,0,1:T(8,128)(2,1)S(1)}, bf16[34,18,128]{2,0,1:T(8,128)(2,1)S(1)}, u32[]{:S(2)}, u32[]{:S(2)}) collective-permute-start(bf16[34,18,128]{2,0,1:T(8,128)(2,1)S(1)} %fusion.39), channel_id=1, source_target_pairs={{0,1},{2,3},{4,5},{6,7},{8,9},{10,11},{12,13},{14,15},{16,17},{18,... | collective-permute-start | bytes 470024 | tf_op jit(solution)/shard_map/ppermute | solution.py:15
  41.4 5.0 %copy-start.10 = (bf16[34,18,128]{2,0,1:T(8,128)(2,1)}, bf16[34,18,128]{2,0,1:T(8,128)(2,1)S(1)}, u32[]{:S(2)}) copy-start(bf16[34,18,128]{2,0,1:T(8,128)(2,1)S(1)} %collective-permute-done.2) | copy-start | bytes 470020
  50.3 1.0 %copy-start.11 = (bf16[34,18,128]{2,0,1:T(8,128)(2,1)S(1)}, bf16[34,18,128]{2,0,1:T(8,128)(2,1)}, u32[]{:S(2)}) copy-start(bf16[34,18,128]{2,0,1:T(8,128)(2,1)} %copy-done.10) | copy-start | bytes 470020
  50.4 0.9 %copy-start.5 = (bf16[18,1,8,17,128]{4,2,3,0,1:T(8,128)(2,1)}, bf16[18,1,8,17,128]{4,2,3,0,1:T(8,128)(2,1)S(1)}, u32[]{:S(2)}) copy-start(bf16[18,1,8,17,128]{4,2,3,0,1:T(8,128)(2,1)S(1)} %copy.32) | copy-start | bytes 1880068
  50.4 3.6 %copy-start.2 = (bf16[9,128,96]{1,2,0:T(8,128)(2,1)S(1)}, bf16[9,128,96]{1,2,0:T(8,128)(2,1)}, u32[]{:S(2)}) copy-start(bf16[9,128,96]{1,2,0:T(8,128)(2,1)} %copy-done.1) | copy-start | bytes 663556
  50.4 3.6 %copy-start.4 = (bf16[9,128,96]{1,2,0:T(8,128)(2,1)S(1)}, bf16[9,128,96]{1,2,0:T(8,128)(2,1)}, u32[]{:S(2)}) copy-start(bf16[9,128,96]{1,2,0:T(8,128)(2,1)} %copy-done.3) | copy-start | bytes 663556
  58.7 1.6 %copy-start.15 = (bf16[3,3,128,224]{2,3,1,0:T(8,128)(2,1)S(1)}, bf16[3,3,128,224]{2,3,1,0:T(8,128)(2,1)}, u32[]{:S(2)}) copy-start(bf16[3,3,128,224]{2,3,1,0:T(8,128)(2,1)} %param.10) | copy-start | bytes 1548292
  58.7 1.6 %copy-start.16 = (pred[8,17]{0,1:T(8,128)(4,1)S(1)}, pred[8,17]{0,1:T(8,128)(4,1)}, u32[]{:S(2)}) copy-start(pred[8,17]{0,1:T(8,128)(4,1)} %constant.94) | copy-start | bytes 412
  60.3 1.3 %copy-start.6 = (bf16[18,1,8,17,128]{4,2,3,0,1:T(8,128)(2,1)S(1)}, bf16[18,1,8,17,128]{4,2,3,0,1:T(8,128)(2,1)}, u32[]{:S(2)}) copy-start(bf16[18,1,8,17,128]{4,2,3,0,1:T(8,128)(2,1)} %copy-done.5) | copy-start | bytes 1880068
  60.3 1.3 %copy-start.12 = (bf16[18,1,7,2,128]{4,2,3,0,1:T(8,128)(2,1)S(1)}, bf16[18,1,7,2,128]{4,2,3,0,1:T(8,128)(2,1)}, u32[]{:S(2)}) copy-start(bf16[18,1,7,2,128]{4,2,3,0,1:T(8,128)(2,1)} %slice.113) | copy-start | bytes 193540
  63.1 0.7 %copy-start.14 = (f32[128]{0:T(128)S(1)}, f32[128]{0:T(128)}, u32[]{:S(2)}) copy-start(f32[128]{0:T(128)} %param.11) | copy-start | bytes 1540
where the time goes:
time: 66.7 us; the launch traced here: 65.3 us
  local copies, waits for them, and re-layouts  27.4 us (41%)
  starting transfers between devices  12.6 us (19%)
  between operations  7.68 us (12%)
  other arithmetic  7.57 us (11%)
  waiting for transfers between devices  6.34 us (10%)
  matrix products  3.76 us (6%)
    ppermute x4, starting transfers between devices, exchange(): return (lax.ppermute(last, axis, up), lax.ppermute(first, axis, down))  12.6 us
    unnamed x43, local copies, waits for them, and re-layouts  12.3 us
    ppermute x4, waiting for transfers between devices, exchange(): return (lax.ppermute(last, axis, up), lax.ppermute(first, axis, down))  6.34 us
    broadcast_in_dim x2, other arithmetic, conv(): block[None]  4.02 us
    conv_general_dilated x6, local copies, waits for them, and re-layouts, conv(): lax.conv_general_dilated(block[None], weight, (1, 1), 'VALID', dimension_...  3.57 us
    conv_general_dilated x2, matrix products, conv(): lax.conv_general_dilated(block[None], weight, (1, 1), 'VALID', dimension_...  2.7 us
    concatenate x1, other arithmetic, body(): jnp.concatenate([left[:, :reach_cols, :depth], source, right[:, :reach_co...  2.09 us
    broadcast_in_dim x2, local copies, waits for them, and re-layouts, conv(): block[None]  1.88 us
  transfers between devices with their start and end apart: 4, of which 2 were waited for; matrix products, arithmetic and copies ran while one was open for 2% of the time, Pallas kernels for 0%

commit v1 on v0

v1 whole, which is shorter than its diff:
```python
import functools

import jax
import jax.numpy as jnp
from jax import lax
from jax.experimental import pallas as pl
from jax.experimental.pallas import tpu as pltpu
from jax.sharding import PartitionSpec as P

MESH = pl.DeviceIdType.MESH
BF = jnp.bfloat16
F32 = jnp.float32
SEG = 32


def pick(ds, positive):
    n = len(ds)
    first, last = jnp.int32(n - 1), jnp.int32(0)
    for k in range(n):
        hit = ds[k] > 0 if positive else ds[k] < 0
        last = jnp.where(hit, jnp.int32(k), last)
    for k in reversed(range(n)):
        hit = ds[k] > 0 if positive else ds[k] < 0
        first = jnp.where(hit, jnp.int32(k), first)
    return first, last


def kernel(
    nr, nc,
    off, hist_hbm, cur_hbm, mix_hbm, cw_ref, bias_ref, out_ref,
    hist, cur, mix, red, rows_all, vsend, hsend, hrecv, csend, cols_all,
    qsend, qrecv, pk, pkrecv, sp, ss, acc, outs, lsem, ssem, rsem,
):
    frames, ch, h, w = hist.shape
    cp = cw_ref.shape[0]
    depth = frames * cp
    reach = h // 2 + 1
    groups = h // 4
    cg = -(-reach // 4)
    own = frames * h
    va, vb = own, own + 2 * reach
    ha, hb = 0, 2 * groups
    ca, cb = 4 * groups, 4 * groups + 2 * cg
    pb, sb = 3 * ch, 3 * depth

    r = lax.axis_index("rows")
    c = lax.axis_index("cols")
    has_up, has_dn, has_lf, has_rt = r > 0, r < nr - 1, c > 0, c < nc - 1
    up_dev, dn_dev, lf_dev, rt_dev = (r - 1, c), (r + 1, c), (r, c - 1), (r, c + 1)

    loads = [pltpu.make_async_copy(hist_hbm.at[k], hist.at[k], lsem.at[k]) for k in range(frames)]
    load_cur = pltpu.make_async_copy(cur_hbm, cur, lsem.at[frames])
    load_mix = pltpu.make_async_copy(mix_hbm, mix, lsem.at[frames + 1])
    for x in (*loads, load_cur, load_mix):
        x.start()

    barrier = pltpu.get_barrier_semaphore()
    for cond, dev in ((has_up, up_dev), (has_dn, dn_dev), (has_lf, lf_dev), (has_rt, rt_dev)):
        @pl.when(cond)
        def _(dev=dev):
            pl.semaphore_signal(barrier, inc=1, device_id=dev, device_id_type=MESH)

    def remote(n, d, src, dst, sideways):
        dev = ((rt_dev, lf_dev) if sideways else (dn_dev, up_dev))[d]
        copy = pltpu.make_async_remote_copy(
            src_ref=src, dst_ref=dst, send_sem=ssem.at[n, d], recv_sem=rsem.at[n, d],
            device_id=dev, device_id_type=MESH,
        )
        ways = (has_rt, has_lf) if sideways else (has_dn, has_up)
        return copy, ways[d], ways[1 - d]

    def start(copies):
        for copy, sends, _ in copies:
            @pl.when(sends)
            def _(copy=copy):
                copy.start()

    def arrive(copies):
        for copy, _, comes in copies:
            @pl.when(comes)
            def _(copy=copy):
                copy.wait_recv()

    def finish(copies):
        for copy, sends, _ in copies:
            @pl.when(sends)
            def _(copy=copy):
                copy.wait_send()

    hcopy = [remote(0, d, hsend.at[d], hrecv.at[pl.ds((ha, hb)[d], 2 * groups)], True) for d in (0, 1)]
    vcopy = [remote(1, d, vsend.at[d], rows_all.at[pl.ds((va, vb)[d], 2 * reach)], False) for d in (0, 1)]
    qcopy = [remote(2, d, qsend, qrecv.at[d], True) for d in (0, 1)]
    pcopy = [
        remote(3, 0, sp.at[pl.ds(h * pb + ch, ch)], sp.at[pl.ds(ch, ch)], False),
        remote(3, 1, sp.at[pl.ds(pb + ch, ch)], sp.at[pl.ds((h + 1) * pb + ch, ch)], False),
    ]
    ccopy = [remote(4, d, csend.at[d], cols_all.at[pl.ds((ca, cb)[d], 2 * cg)], False) for d in (0, 1)]
    kcopy = [remote(5, d, pk, pkrecv.at[d], False) for d in (0, 1)]

    dys = [off[k, 0] for k in range(frames)]
    dxs = [off[k, 1] for k in range(frames)]
    down, up = pick(dys, True), pick(dys, False)
    right, left = pick(dxs, True), pick(dxs, False)

    def slot(k, d, plus, minus):
        other = jnp.where(d > 0, plus[0], minus[0]) != k
        return jnp.where(other, jnp.int32(1), jnp.int32(0))

    vslot = [slot(k, dys[k], down, up) for k in range(frames)]
    hslot = [slot(k, dxs[k], right, left) for k in range(frames)]
    side = [jnp.where(dxs[k] > 0, ha, hb) + hslot[k] * groups for k in range(frames)]

    def clear(ref, first, size):
        ref[pl.ds(first, size)] = jnp.zeros((size, *ref.shape[1:]), BF)

    @pl.when(r == 0)
    def _():
        clear(rows_all, va, 2 * reach)
        clear(cols_all, ca, 2 * cg)
        clear(pkrecv, 0, 1)
        clear(sp, ch, ch)

    @pl.when(r == nr - 1)
    def _():
        clear(rows_all, vb, 2 * reach)
        clear(cols_all, cb, 2 * cg)
        clear(pkrecv, 1, 1)
        clear(sp, (h + 1) * pb + ch, ch)

    @pl.when(c == 0)
    def _():
        clear(hrecv, ha, 2 * groups)
        clear(qrecv, 0, 1)

    @pl.when(c == nc - 1)
    def _():
        clear(hrecv, hb, 2 * groups)
        clear(qrecv, 1, 1)

    for k in range(frames):
        loads[k].wait()
        rows = jnp.swapaxes(hist[k], 0, 1)
        for y in range(0, h, 2):
            rhs = jnp.concatenate([rows[y], rows[y + 1]], axis=1)
            got = jnp.dot(cw_ref[...], rhs, preferred_element_type=F32).astype(BF)
            for e in (0, 1):
                part = got[:, e * w:(e + 1) * w]
                red[k * h + y + e] = part
                rows_all[k * h + y + e] = part

    lane = lax.broadcasted_iota(jnp.int32, (cp, w), 1)
    for d in (0, 1):
        for s in (0, 1):
            frame, base = (right[s], SEG) if d == 0 else (left[s], 0)
            for g in range(groups):
                tile = None
                for q in range(4):
                    row = red[frame * h + 4 * g + q]
                    turn = (base + SEG * q) % w
                    row = pltpu.roll(row, turn, 1) if turn else row
                    tile = row if tile is None else jnp.where(lane >= SEG * q, row, tile)
                hsend[d, s * groups + g] = tile

    count = sum(jnp.where(x, jnp.int32(1), jnp.int32(0)) for x in (has_up, has_dn, has_lf, has_rt))
    pl.semaphore_wait(barrier, count)
    start(hcopy)
    for s in (0, 1):
        vsend[0, pl.ds(s * reach, reach)] = red[pl.ds(down[s] * h + h - reach, reach)]
        vsend[1, pl.ds(s * reach, reach)] = red[pl.ds(up[s] * h, reach)]
    start(vcopy)

    load_cur.wait()
    rows = jnp.swapaxes(cur[...], 0, 1)
    for y in range(h):
        sp[pl.ds((y + 1) * pb + ch, ch)] = rows[y]
    start(pcopy)
    lane_c = lax.broadcasted_iota(jnp.int32, (ch, w), 1)
    tile = jnp.zeros((ch, w), BF)
    for t in range(1, h + 1):
        turned = pltpu.roll(rows[t - 1], 2 * t + 2, 1)
        tile = jnp.where((lane_c >= 2 * t + 1) & (lane_c <= 2 * t + 2), turned, tile)
    qsend[...] = tile
    start(qcopy)

    load_mix.wait()
    wp = jnp.concatenate([mix[i, j, :, :ch] for i in range(3) for j in range(3)], axis=1)
    fill = jnp.zeros((ch, w - depth), BF)
    taps = [jnp.concatenate([mix[i, j, :, ch:], fill], axis=1) for i in range(3) for j in range(3)]
    extra = [(tap, f) for tap in (6, 7) for f in range(frames)]
    tiles, order = [], []
    for n in range(6):
        tap, f = extra[n]
        turned = pltpu.roll(taps[tap], w - cp - f * cp, 1)
        tiles.append(jnp.where(lane_c >= depth, turned, taps[n]))
        order += [(n, g) for g in range(frames)] + [(tap, f)]
    tiles.append(taps[8])
    order += [(8, g) for g in range(frames)] + [(8, 0)]
    ws = jnp.concatenate(tiles, axis=1)
    wide = jnp.broadcast_to(bias_ref[...][None, :], (ch, ch))
    eye = lax.broadcasted_iota(jnp.int32, (ch, ch), 0) == lax.broadcasted_iota(jnp.int32, (ch, ch), 1)
    bias = jnp.sum(jnp.where(eye, wide, 0.0), axis=1, keepdims=True)

    arrive(qcopy)
    edge = jnp.where((lane_c & 1) == 1, qrecv[0], pltpu.roll(qrecv[1], w - 2, 1))
    pk[...] = edge
    start(kcopy)
    arrive(hcopy)
    for s in (0, 1):
        for d, frame in ((0, down[s]), (1, up[s])):
            base = jnp.int32(0)
            for k in range(frames):
                base = jnp.where(frame == k, side[k], base)
            first = base + (groups - cg if d == 0 else 0)
            csend[d, pl.ds(s * cg, cg)] = hrecv[pl.ds(first, cg)]
    start(ccopy)
    cols_all[pl.ds(0, 4 * groups)] = hrecv[...]

    def widen(t, edge):
        mid = sp[pl.ds(t * pb + ch, ch)]
        ends = pltpu.roll(edge, w - 2 * t - 1, 1)
        sp[pl.ds(t * pb, ch)] = jnp.where(lane_c == 0, ends, pltpu.roll(mid, 1, 1))
        sp[pl.ds(t * pb + 2 * ch, ch)] = jnp.where(lane_c == w - 1, ends, pltpu.roll(mid, w - 1, 1))

    def present(p):
        y = 2 * p
        rhs = jnp.concatenate([sp[pl.ds(y * pb, 3 * pb)], sp[pl.ds((y + 1) * pb, 3 * pb)]], axis=1)
        acc[p] = jnp.dot(wp, rhs, preferred_element_type=F32)

    for t in range(1, h + 1):
        widen(t, edge)
    for p in range(1, h // 2 - 1):
        present(p)
    arrive(pcopy)
    arrive(kcopy)
    edge = jnp.where(
        lane_c < 2, pltpu.roll(pkrecv[0], w - 2 * h, 1), pltpu.roll(pkrecv[1], 2 * h, 1)
    )
    widen(0, edge)
    widen(h + 1, edge)
    present(0)
    present(h // 2 - 1)

    arrive(vcopy)
    arrive(ccopy)
    for k in range(frames):
        dy, dx = dys[k], dxs[k]
        plus = dx > 0
        lo = jnp.where(plus, 0, w + dx)
        hi = jnp.where(plus, dx, w)
        flag = jnp.where(plus, jnp.int32(1), jnp.int32(0))
        base = jnp.where((lane >= lo) & (lane < hi), jnp.int32(1), jnp.int32(0))
        mid_m = base == 1
        lo_m = jnp.where(lane == w - 1, flag, base) == 1
        hi_m = jnp.where(lane == 0, 1 - flag, base) == 1
        lf_out = (lane == 0) & (c == 0)
        rt_out = (lane == w - 1) & (c == nc - 1)
        own_turn = lax.rem(dx + w, w)
        halo_turn = dx - jnp.where(plus, SEG, 0)
        for t in range(h + 2):
            y = t - 1 - dy
            above, below = y < 0, y >= h
            at = jnp.where(
                above, va + vslot[k] * reach + y + reach,
                jnp.where(below, vb + vslot[k] * reach + y - h, k * h + y),
            )
            near = jnp.where(above, y + h, jnp.where(below, y - h, y))
            quad = lax.shift_right_logical(near, jnp.int32(2))
            col = jnp.where(
                above, ca + vslot[k] * cg + quad - (groups - cg),
                jnp.where(below, cb + vslot[k] * cg + quad, side[k] + quad),
            )
            turn = lax.rem(halo_turn - SEG * (near & 3) + 2 * w, w)
            mine = pltpu.roll(rows_all[at], own_turn, 1)
            theirs = pltpu.roll(cols_all[col], turn, 1)
            place = t * sb + k * cp
            lf = pltpu.roll(jnp.where(lo_m, theirs, mine), 1, 1)
            rt = pltpu.roll(jnp.where(hi_m, theirs, mine), w - 1, 1)
            ss[pl.ds(place, cp)] = jnp.where(lf_out, jnp.zeros_like(lf), lf)
            ss[pl.ds(place + depth, cp)] = jnp.where(mid_m, theirs, mine)
            ss[pl.ds(place + 2 * depth, cp)] = jnp.where(rt_out, jnp.zeros_like(rt), rt)

    @pl.when(r == 0)
    def _():
        clear(ss, 0, sb)

    @pl.when(r == nr - 1)
    def _():
        clear(ss, (h + 1) * sb, sb)

    for p in range(h // 2):
        halves = []
        for y in (2 * p, 2 * p + 1):
            halves.append(jnp.concatenate(
                [ss[pl.ds((y + tap // 3) * sb + (tap % 3) * depth + f * cp, cp)] for tap, f in order], axis=0
            ))
        total = acc[p] + jnp.dot(ws, jnp.concatenate(halves, axis=1), preferred_element_type=F32)
        total = jnp.maximum(total + bias, 0.0).astype(BF)
        outs[2 * p] = total[:, :w]
        outs[2 * p + 1] = total[:, w:]
    out_ref[...] = jnp.swapaxes(outs[...], 0, 1)

    for copies in (hcopy, vcopy, qcopy, pcopy, ccopy, kcopy):
        finish(copies)


def body(nr, nc, current_frame, history_frames, offsets, compress_weight, mixer_weight, mixer_bias):
    frames, ch, h, w = history_frames.shape
    cp = compress_weight.shape[0]
    depth = frames * cp
    reach = h // 2 + 1
    groups = h // 4
    cg = -(-reach // 4)
    anyspace = pl.BlockSpec(memory_space=pl.ANY)
    vmem = pl.BlockSpec(memory_space=pltpu.VMEM)
    return pl.pallas_call(
        functools.partial(kernel, nr, nc),
        out_shape=jax.ShapeDtypeStruct((ch, h, w), BF),
        in_specs=[pl.BlockSpec(memory_space=pltpu.SMEM), anyspace, anyspace, anyspace, vmem, vmem],
        out_specs=vmem,
        scratch_shapes=[
            pltpu.VMEM((frames, ch, h, w), BF),
            pltpu.VMEM((ch, h, w), BF),
            pltpu.VMEM(mixer_weight.shape, BF),
            pltpu.VMEM((frames * h, cp, w), BF),
            pltpu.VMEM((frames * h + 4 * reach, cp, w), BF),
            pltpu.VMEM((2, 2 * reach, cp, w), BF),
            pltpu.VMEM((2, 2 * groups, cp, w), BF),
            pltpu.VMEM((4 * groups, cp, w), BF),
            pltpu.VMEM((2, 2 * cg, cp, w), BF),
            pltpu.VMEM((4 * groups + 4 * cg, cp, w), BF),
            pltpu.VMEM((ch, w), BF),
            pltpu.VMEM((2, ch, w), BF),
            pltpu.VMEM((ch, w), BF),
            pltpu.VMEM((2, ch, w), BF),
            pltpu.VMEM(((h + 2) * 3 * ch, w), BF),
            pltpu.VMEM(((h + 2) * 3 * depth, w), BF),
            pltpu.VMEM((h // 2, ch, 2 * w), F32),
            pltpu.VMEM((h, ch, w), BF),
            pltpu.SemaphoreType.DMA((frames + 2,)),
            pltpu.SemaphoreType.DMA((6, 2)),
            pltpu.SemaphoreType.DMA((6, 2)),
        ],
        compiler_params=pltpu.CompilerParams(collective_id=0, has_side_effects=True),
        name="join",
    )(offsets, history_frames, current_frame, mixer_weight, compress_weight, mixer_bias)


def solution(mesh):
    in_specs = (P(None, "rows", "cols"), P(None, None, "rows", "cols"), P(), P(), P(), P())
    out_specs = P(None, "rows", "cols")
    return jax.shard_map(
        functools.partial(body, mesh.shape["rows"], mesh.shape["cols"]),
        mesh=mesh, in_specs=in_specs, out_specs=out_specs, check_vma=False,
    )
```

time: 66.7 us -> 22.3 us (0.33); the launches traced: 65.3 us -> 22.1 us
  local copies, waits for them, and re-layouts: 27.4 us -> 5.29 us
  Pallas kernels: 0 us -> 16.8 us
  starting transfers between devices: 12.6 us -> 0 us
  between operations: 7.68 us -> 0.01 us
  other arithmetic: 7.57 us -> 0 us
  waiting for transfers between devices: 6.34 us -> 0 us
  matrix products: 3.76 us -> 0 us
    pallas_call x0 -> x1, Pallas kernels: none -> 16.8 us  [body(): pl.pallas_call(functools.partial(kernel, nr, nc), out_shape=jax.ShapeDtyp...]
    ppermute x4 -> x0, starting transfers between devices: 12.6 us -> none  [exchange(): return (lax.ppermute(last, axis, up), lax.ppermute(first, axis, down))]
    slice x15 -> x0, local copies, waits for them, and re-layouts: 7.99 us -> none  [the longest x2 1.8 us: body(): right[:height + 2, reach_cols:, :channels]]
    unnamed x43 -> x3, local copies, waits for them, and re-layouts: 12.3 us -> 5.29 us
    ppermute x4 -> x0, waiting for transfers between devices: 6.34 us -> none  [exchange(): return (lax.ppermute(last, axis, up), lax.ppermute(first, axis, down))]
    broadcast_in_dim x2 -> x0, other arithmetic: 4.02 us -> none  [conv(): block[None]]
    conv_general_dilated x6 -> x0, local copies, waits for them, and re-layouts: 3.57 us -> none  [conv(): lax.conv_general_dilated(block[None], weight, (1, 1), 'VALID', dimension_...]
    concatenate x7 -> x0, other arithmetic: 3.35 us -> none  [the longest x1 2.09 us: body(): jnp.concatenate([left[:, :reach_cols, :depth], source, right[:, :reach_co...]
  transfers between devices with their start and end apart: 4 -> 0, of which waited for: 2 -> 0; matrix products, arithmetic and copies ran while one was open for 2% -> 0% of each run, Pallas kernels for 0% -> 0%
where the time goes in v1:
time: 22.3 us; the launch traced here: 22.1 us
  Pallas kernels  16.8 us (75%)
  local copies, waits for them, and re-layouts  5.29 us (24%)
    pallas_call x1, Pallas kernels, body(): pl.pallas_call(functools.partial(kernel, nr, nc), out_shape=jax.ShapeDtyp...  16.8 us
    unnamed x3, local copies, waits for them, and re-layouts  5.29 us

profile of v1, /device:TPU:1, one launch (start us, length us, event | category | flops | bytes accessed | tf_op | source)
XLA Modules:
  0.0 22.1 jit_solution(17344563700887438041)
XLA Ops:
  0.0 1.3 %copy.7.off = s32[3,2]{1,0:T(4,128)} copy(s32[3,2]{0,1:T(2,128)} %param.8) | data formatting | bytes 48 | tf_op args[2]
  1.3 2.1 %copy.8.mix_hbm = bf16[3,3,128,224]{3,2,1,0:T(8,128)(2,1)} copy(bf16[3,3,128,224]{2,3,1,0:T(8,128)(2,1)} %param.10) | data formatting | bytes 1032192 | tf_op args[4]
  3.4 16.8 %join.1 = bf16[128,16,128]{2,1,0:T(8,128)(2,1)} custom-call(s32[3,2]{1,0:T(4,128)} %copy.7.off, bf16[3,128,16,128]{3,2,1,0:T(8,128)(2,1)} %hist_hbm.1, bf16[128,16,128]{2,1,0:T(8,128)(2,1)} %cur_hbm.1, bf16[3,3,128,224]{3,2,1,0:T(8,128)(2,1)} %copy.8.mix_hbm, bf16[32,128]{1,0:T(8,128)(2,1)} %cw_ref.1, f32[128]{0:T(128)} %bias_ref.1), custom_call_target="tpu_custom_call" | custom-call | tf_op jit(solution)/shard_map/join/pallas_call | solution.py:315
  20.2 1.9 %copy.10 = bf16[128,16,128]{2,1,0:T(8,128)(2,1)} copy(bf16[128,16,128]{2,1,0:T(8,128)(2,1)} %join.1) | data formatting | bytes 1048576

commit v2 on v1

--- a/solution.py
+++ b/solution.py
@@ -29,7 +29,7 @@
     nr, nc,
     off, hist_hbm, cur_hbm, mix_hbm, cw_ref, bias_ref, out_ref,
     hist, cur, mix, red, rows_all, vsend, hsend, hrecv, csend, cols_all,
-    qsend, qrecv, pk, pkrecv, sp, ss, acc, outs, lsem, ssem, rsem,
+    qsend, qrecv, pk, pkrecv, sp, ss, acc, wp, ws, lsem, ssem, rsem,
 ):
     frames, ch, h, w = hist.shape
     cp = cw_ref.shape[0]
@@ -97,8 +97,8 @@
     ccopy = [remote(4, d, csend.at[d], cols_all.at[pl.ds((ca, cb)[d], 2 * cg)], False) for d in (0, 1)]
     kcopy = [remote(5, d, pk, pkrecv.at[d], False) for d in (0, 1)]
 
-    dys = [off[k, 0] for k in range(frames)]
-    dxs = [off[k, 1] for k in range(frames)]
+    dys = [off[0, k] for k in range(frames)]
+    dxs = [off[1, k] for k in range(frames)]
     down, up = pick(dys, True), pick(dys, False)
     right, left = pick(dxs, True), pick(dxs, False)
 
@@ -183,19 +183,14 @@
     start(qcopy)
 
     load_mix.wait()
-    wp = jnp.concatenate([mix[i, j, :, :ch] for i in range(3) for j in range(3)], axis=1)
-    fill = jnp.zeros((ch, w - depth), BF)
-    taps = [jnp.concatenate([mix[i, j, :, ch:], fill], axis=1) for i in range(3) for j in range(3)]
-    extra = [(tap, f) for tap in (6, 7) for f in range(frames)]
-    tiles, order = [], []
-    for n in range(6):
-        tap, f = extra[n]
-        turned = pltpu.roll(taps[tap], w - cp - f * cp, 1)
-        tiles.append(jnp.where(lane_c >= depth, turned, taps[n]))
-        order += [(n, g) for g in range(frames)] + [(tap, f)]
-    tiles.append(taps[8])
-    order += [(8, g) for g in range(frames)] + [(8, 0)]
-    ws = jnp.concatenate(tiles, axis=1)
+    for i in range(3):
+        for j in range(3):
+            wp[:, (3 * i + j) * ch:(3 * i + j + 1) * ch] = jnp.swapaxes(mix[i, j, :ch], 0, 1)
+    past = [mix[i, j, ch:] for i in range(3) for j in range(3)]
+    past.append(jnp.zeros((ws.shape[1] - 9 * depth, ch), BF))
+    past = jnp.concatenate(past, axis=0)
+    for n in range(0, ws.shape[1], ch):
+        ws[:, n:n + ch] = jnp.swapaxes(past[n:n + ch], 0, 1)
     wide = jnp.broadcast_to(bias_ref[...][None, :], (ch, ch))
     eye = lax.broadcasted_iota(jnp.int32, (ch, ch), 0) == lax.broadcasted_iota(jnp.int32, (ch, ch), 1)
     bias = jnp.sum(jnp.where(eye, wide, 0.0), axis=1, keepdims=True)
@@ -224,7 +219,7 @@
     def present(p):
         y = 2 * p
         rhs = jnp.concatenate([sp[pl.ds(y * pb, 3 * pb)], sp[pl.ds((y + 1) * pb, 3 * pb)]], axis=1)
-        acc[p] = jnp.dot(wp, rhs, preferred_element_type=F32)
+        acc[p] = jnp.dot(wp[...], rhs, preferred_element_type=F32)
 
     for t in range(1, h + 1):
         widen(t, edge)
@@ -287,20 +282,23 @@
     def _():
         clear(ss, (h + 1) * sb, sb)
 
+    lead = ws.shape[1] - 9 * depth
     for p in range(h // 2):
         halves = []
         for y in (2 * p, 2 * p + 1):
-            halves.append(jnp.concatenate(
-                [ss[pl.ds((y + tap // 3) * sb + (tap % 3) * depth + f * cp, cp)] for tap, f in order], axis=0
-            ))
-        total = acc[p] + jnp.dot(ws, jnp.concatenate(halves, axis=1), preferred_element_type=F32)
+            rows = ss[pl.ds(y * sb, 3 * sb)]
+            halves.append(jnp.concatenate([rows, rows[:lead]], axis=0))
+        total = acc[p] + jnp.dot(ws[...], jnp.concatenate(halves, axis=1), preferred_element_type=F32)
         total = jnp.maximum(total + bias, 0.0).astype(BF)
-        outs[2 * p] = total[:, :w]
-        outs[2 * p + 1] = total[:, w:]
-    out_ref[...] = jnp.swapaxes(outs[...], 0, 1)
+        out_ref[2 * p] = total[:, :w]
+        out_ref[2 * p + 1] = total[:, w:]
 
     for copies in (hcopy, vcopy, qcopy, pcopy, ccopy, kcopy):
         finish(copies)
+
+
+def place(rows_ref, out_ref):
+    out_ref[...] = jnp.swapaxes(rows_ref[...], 0, 1)
 
 
 def body(nr, nc, current_frame, history_frames, offsets, compress_weight, mixer_weight, mixer_bias):
@@ -310,17 +308,18 @@
     reach = h // 2 + 1
     groups = h // 4
     cg = -(-reach // 4)
+    mix = mixer_weight.transpose(0, 1, 3, 2)
     anyspace = pl.BlockSpec(memory_space=pl.ANY)
     vmem = pl.BlockSpec(memory_space=pltpu.VMEM)
-    return pl.pallas_call(
+    joined = pl.pallas_call(
         functools.partial(kernel, nr, nc),
-        out_shape=jax.ShapeDtypeStruct((ch, h, w), BF),
+        out_shape=pltpu.VMEM((h, ch, w), BF),
         in_specs=[pl.BlockSpec(memory_space=pltpu.SMEM), anyspace, anyspace, anyspace, vmem, vmem],
         out_specs=vmem,
         scratch_shapes=[
             pltpu.VMEM((frames, ch, h, w), BF),
             pltpu.VMEM((ch, h, w), BF),
-            pltpu.VMEM(mixer_weight.shape, BF),
+            pltpu.VMEM(mix.shape, BF),
             pltpu.VMEM((frames * h, cp, w), BF),
             pltpu.VMEM((frames * h + 4 * reach, cp, w), BF),
             pltpu.VMEM((2, 2 * reach, cp, w), BF),
@@ -335,14 +334,22 @@
             pltpu.VMEM(((h + 2) * 3 * ch, w), BF),
             pltpu.VMEM(((h + 2) * 3 * depth, w), BF),
             pltpu.VMEM((h // 2, ch, 2 * w), F32),
-            pltpu.VMEM((h, ch, w), BF),
+            pltpu.VMEM((ch, 9 * ch), BF),
+            pltpu.VMEM((ch, -(-9 * depth // 128) * 128), BF),
             pltpu.SemaphoreType.DMA((frames + 2,)),
             pltpu.SemaphoreType.DMA((6, 2)),
             pltpu.SemaphoreType.DMA((6, 2)),
         ],
         compiler_params=pltpu.CompilerParams(collective_id=0, has_side_effects=True),
         name="join",
-    )(offsets, history_frames, current_frame, mixer_weight, compress_weight, mixer_bias)
+    )(offsets.T, history_frames, current_frame, mix, compress_weight, mixer_bias)
+    return pl.pallas_call(
+        place,
+        out_shape=jax.ShapeDtypeStruct((ch, h, w), BF),
+        in_specs=[vmem],
+        out_specs=vmem,
+        name="place",
+    )(pltpu.with_memory_space_constraint(joined, pltpu.VMEM))
 
 
 def solution(mesh):

time: 22.3 us -> 17.1 us (0.77)
  local copies, waits for them, and re-layouts: 5.29 us -> 0 us
    unnamed x3 -> x0, local copies, waits for them, and re-layouts: 5.29 us -> none
    pallas_call x1 -> x2, Pallas kernels: 16.8 us -> 16.9 us  [the longest x1 16 us: body(): pl.pallas_call(functools.partial(kernel, nr, nc), out_shape=pltpu.VMEM((h...]
where the time goes in v2:
time: 17.1 us; the launch traced here: 16.9 us
  Pallas kernels  16.9 us (99%)
    pallas_call x1, Pallas kernels, body(): pl.pallas_call(functools.partial(kernel, nr, nc), out_shape=pltpu.VMEM((h...  16 us
    pallas_call x1, Pallas kernels, body(): pl.pallas_call(place, out_shape=jax.ShapeDtypeStruct((ch, h, w), BF), in_...  0.93 us

profile of v2, /device:TPU:1, one launch (start us, length us, event | category | flops | bytes accessed | tf_op | source)
XLA Modules:
  0.0 16.9 jit_solution(4684097931345660099)
XLA Ops:
  0.0 16.0 %join.1.rows_ref = bf16[16,128,128]{2,1,0:T(8,128)(2,1)S(1)} custom-call(s32[2,3]{1,0:T(2,128)} %bitcast.3, bf16[3,128,16,128]{3,2,1,0:T(8,128)(2,1)} %hist_hbm.1, bf16[128,16,128]{2,1,0:T(8,128)(2,1)} %cur_hbm.1, bf16[3,3,224,128]{3,2,1,0:T(8,128)(2,1)} %bitcast.2, bf16[32,128]{1,0:T(8,128)(2,1)} %cw_ref.1, f32[128]{0:T(128)} %bias_ref.1), custom_call_target="tpu_custom_call" | custom-call | tf_op jit(solution)/shard_map/join/pallas_call | solution.py:314
  16.0 0.9 %place.1 = bf16[128,16,128]{2,1,0:T(8,128)(2,1)} custom-call(bf16[16,128,128]{2,1,0:T(8,128)(2,1)S(1)} %join.1.rows_ref), custom_call_target="tpu_custom_call" | custom-call | tf_op jit(solution)/shard_map/place/pallas_call | solution.py:346

commit v3 on v2

v3 whole, which is shorter than its diff:
```python
import functools

import jax
import jax.numpy as jnp
from jax import lax
from jax.experimental import pallas as pl
from jax.experimental.pallas import tpu as pltpu
from jax.sharding import PartitionSpec as P

MESH = pl.DeviceIdType.MESH
BF = jnp.bfloat16
F32 = jnp.float32
PACK = 7
REACH_X = 17


def pick(ds, positive):
    n = len(ds)
    first, last = jnp.int32(n - 1), jnp.int32(0)
    for k in range(n):
        hit = ds[k] > 0 if positive else ds[k] < 0
        last = jnp.where(hit, jnp.int32(k), last)
    for k in reversed(range(n)):
        hit = ds[k] > 0 if positive else ds[k] < 0
        first = jnp.where(hit, jnp.int32(k), first)
    return first, last


def kernel(
    nr, nc,
    off, hist_hbm, cur_hbm, mix_hbm, cw_ref, bias_ref, out_ref,
    hist, cur, mix, red, vsend, vrecv, hsend, hrecv, csend, crecv,
    qfull, qsend, qrecv, krecv, pk, sp, unp, xs, acc, wp, ws, lsem, ssem, rsem,
):
    frames, ch, h, w = hist.shape
    cp = cw_ref.shape[0]
    depth = frames * cp
    reach = h // 2 + 1
    ring = h + reach
    pitch = w // PACK
    tiles = -(-h // PACK)
    ctiles = -(-reach // PACK)
    pb = 3 * ch
    quarter = ch // 4

    r = lax.axis_index("rows")
    c = lax.axis_index("cols")
    has_up, has_dn, has_lf, has_rt = r > 0, r < nr - 1, c > 0, c < nc - 1
    up_dev, dn_dev, lf_dev, rt_dev = (r - 1, c), (r + 1, c), (r, c - 1), (r, c + 1)

    loads = [pltpu.make_async_copy(hist_hbm.at[k], hist.at[k], lsem.at[k]) for k in range(frames)]
    load_cur = pltpu.make_async_copy(cur_hbm, cur, lsem.at[frames])
    load_mix = pltpu.make_async_copy(mix_hbm, mix, lsem.at[frames + 1])
    for x in (*loads, load_cur, load_mix):
        x.start()

    barrier = pltpu.get_barrier_semaphore()
    for cond, dev in ((has_up, up_dev), (has_dn, dn_dev), (has_lf, lf_dev), (has_rt, rt_dev)):
        @pl.when(cond)
        def _(dev=dev):
            pl.semaphore_signal(barrier, inc=1, device_id=dev, device_id_type=MESH)

    def remote(n, d, src, dst, sideways):
        dev = ((rt_dev, lf_dev) if sideways else (dn_dev, up_dev))[d]
        copy = pltpu.make_async_remote_copy(
            src_ref=src, dst_ref=dst, send_sem=ssem.at[n, d], recv_sem=rsem.at[n, d],
            device_id=dev, device_id_type=MESH,
        )
        ways = (has_rt, has_lf) if sideways else (has_dn, has_up)
        return copy, ways[d], ways[1 - d]

    def start(copies):
        for copy, sends, _ in copies:
            @pl.when(sends)
            def _(copy=copy):
                copy.start()

    def arrive(copies):
        for copy, _, comes in copies:
            @pl.when(comes)
            def _(copy=copy):
                copy.wait_recv()

    def finish(copies):
        for copy, sends, _ in copies:
            @pl.when(sends)
            def _(copy=copy):
                copy.wait_send()

    hcopy = [remote(0, d, hsend.at[d], hrecv.at[d], True) for d in (0, 1)]
    vcopy = [remote(1, d, vsend.at[d], vrecv.at[d], False) for d in (0, 1)]
    qcopy = [remote(2, d, qsend, qrecv.at[d], True) for d in (0, 1)]
    pcopy = [
        remote(3, 0, sp.at[pl.ds(h * pb + ch, ch)], sp.at[pl.ds(ch, ch)], False),
        remote(3, 1, sp.at[pl.ds(pb + ch, ch)], sp.at[pl.ds((h + 1) * pb + ch, ch)], False),
    ]
    ccopy = [remote(4, d, csend.at[d], crecv.at[d], False) for d in (0, 1)]
    kcopy = [remote(5, d, qrecv, krecv.at[d], False) for d in (0, 1)]

    dys = [off[0, k] for k in range(frames)]
    dxs = [off[1, k] for k in range(frames)]
    down, up = pick(dys, True), pick(dys, False)
    right, left = pick(dxs, True), pick(dxs, False)

    def slot(k, d, plus, minus):
        other = jnp.where(d > 0, plus[0], minus[0]) != k
        return jnp.where(other, jnp.int32(1), jnp.int32(0))

    vslot = [slot(k, dys[k], down, up) for k in range(frames)]
    hslot = [slot(k, dxs[k], right, left) for k in range(frames)]
    went_x = [jnp.where(dxs[k] > 0, jnp.int32(0), jnp.int32(1)) for k in range(frames)]
    went_y = [jnp.where(dys[k] > 0, jnp.int32(0), jnp.int32(1)) for k in range(frames)]

    def clear(ref):
        ref[...] = jnp.zeros(ref.shape, BF)

    @pl.when(r == 0)
    def _():
        for ref in (vrecv.at[0], crecv.at[0], krecv.at[0], sp.at[pl.ds(ch, ch)]):
            clear(ref)

    @pl.when(r == nr - 1)
    def _():
        for ref in (vrecv.at[1], crecv.at[1], krecv.at[1], sp.at[pl.ds((h + 1) * pb + ch, ch)]):
            clear(ref)

    @pl.when(c == 0)
    def _():
        clear(hrecv.at[0])
        clear(qrecv.at[0])

    @pl.when(c == nc - 1)
    def _():
        clear(hrecv.at[1])
        clear(qrecv.at[1])

    for k in range(frames):
        loads[k].wait()
        rows = jnp.swapaxes(hist[k], 0, 1)
        for y in range(0, h, 2):
            rhs = jnp.concatenate([rows[y], rows[y + 1]], axis=1)
            got = jnp.dot(cw_ref[...], rhs, preferred_element_type=F32).astype(BF)
            for e in (0, 1):
                red[k * h + y + e] = got[:, e * w:(e + 1) * w]

    lane = lax.broadcasted_iota(jnp.int32, (cp, w), 1)
    for d in (0, 1):
        for s in (0, 1):
            frame, base = (right[s], REACH_X) if d == 0 else (left[s], 0)
            for g in range(tiles):
                tile = None
                for q in range(min(PACK, h - PACK * g)):
                    row = red[frame * h + PACK * g + q]
                    turn = (base + pitch * q) % w
                    row = pltpu.roll(row, turn, 1) if turn else row
                    tile = row if tile is None else jnp.where(lane >= pitch * q, row, tile)
                hsend[d, s * tiles + g] = tile

    count = sum(jnp.where(x, jnp.int32(1), jnp.int32(0)) for x in (has_up, has_dn, has_lf, has_rt))
    pl.semaphore_wait(barrier, count)
    start(hcopy)
    for s in (0, 1):
        vsend[0, pl.ds(s * reach, reach)] = red[pl.ds(down[s] * h + h - reach, reach)]
        vsend[1, pl.ds(s * reach, reach)] = red[pl.ds(up[s] * h, reach)]
    start(vcopy)

    load_cur.wait()
    rows = jnp.swapaxes(cur[...], 0, 1)
    for y in range(h):
        sp[pl.ds((y + 1) * pb + ch, ch)] = rows[y]
    start(pcopy)
    lane_c = lax.broadcasted_iota(jnp.int32, (ch, w), 1)
    tile = jnp.zeros((ch, w), BF)
    for y in range(h):
        turned = pltpu.roll(rows[y], 2 * y + 1, 1)
        tile = jnp.where((lane_c == 2 * y) | (lane_c == 2 * y + 1), turned, tile)
    qfull[...] = tile
    small = qfull[pl.ds(0, quarter)]
    lane_q = lax.broadcasted_iota(jnp.int32, (quarter, w), 1)
    for g in range(1, 4):
        turned = pltpu.roll(qfull[pl.ds(g * quarter, quarter)], 2 * h * g, 1)
        small = jnp.where(lane_q >= 2 * h * g, turned, small)
    qsend[...] = small
    start(qcopy)

    load_mix.wait()
    for i in range(3):
        for j in range(3):
            wp[:, (3 * i + j) * ch:(3 * i + j + 1) * ch] = jnp.swapaxes(mix[i, j, :ch], 0, 1)
    past = [
        mix[i, j, ch + k * cp:ch + (k + 1) * cp] for i in range(3) for k in range(frames) for j in range(3)
    ]
    lead = ws.shape[1] - 9 * depth
    past.append(jnp.zeros((lead, ch), BF))
    past = jnp.concatenate(past, axis=0)
    for n in range(0, ws.shape[1], ch):
        ws[:, n:n + ch] = jnp.swapaxes(past[n:n + ch], 0, 1)
    wide = jnp.broadcast_to(bias_ref[...][None, :], (ch, ch))
    eye = lax.broadcasted_iota(jnp.int32, (ch, ch), 0) == lax.broadcasted_iota(jnp.int32, (ch, ch), 1)
    bias = jnp.sum(jnp.where(eye, wide, 0.0), axis=1, keepdims=True)

    arrive(hcopy)
    for s in (0, 1):
        for d, frame in ((0, down[s]), (1, up[s])):
            way, at = jnp.int32(0), jnp.int32(0)
            for k in range(frames):
                way = jnp.where(frame == k, went_x[k], way)
                at = jnp.where(frame == k, hslot[k] * tiles, at)
            first = at + (tiles - ctiles if d == 0 else 0)
            csend[d, pl.ds(s * ctiles, ctiles)] = hrecv[way, pl.ds(first, ctiles)]
    start(ccopy)
    arrive(qcopy)
    start(kcopy)

    def ends(near, lf_turn, rt_turn):
        lf = jnp.concatenate(
            [pltpu.roll(near[0], (2 * w - 2 * h * g - lf_turn) % w, 1) for g in range(4)], axis=0
        )
        rt = jnp.concatenate(
            [pltpu.roll(near[1], (2 * w - 2 * h * g - rt_turn) % w, 1) for g in range(4)], axis=0
        )
        return jnp.where((lane_c & 1) == 0, lf, rt)

    pk[...] = ends(qrecv, 0, 2)

    masks, kills = [], []
    for k in range(frames):
        plus = dxs[k] > 0
        mine, dead = [], []
        for j in range(3):
            step = dxs[k] + 1 - j
            lo = jnp.where(plus, w - step, 0)
            hi = jnp.where(plus, w, -step)
            mine.append((lane >= lo) & (lane < hi))
            at = jnp.int32(-1)
            if j == 0:
                at = jnp.where(plus | (c > 0), at, -step)
            if j == 2:
                at = jnp.where(plus & (c == nc - 1), w - 1 - step, at)
            dead.append(lane == at)
        masks.append(mine)
        kills.append(dead)

    def unpack(k, m, q, tile):
        turn = (jnp.where(dxs[k] > 0, w - REACH_X, 0) - pitch * q + w) & (w - 1)
        unp[k * ring + m] = pltpu.roll(tile, turn, 1)

    def shift(k, m, row):
        far = unp[k * ring + m]
        for j in range(3):
            near = row if j == 1 else jnp.where(kills[k][j], jnp.zeros_like(row), row)
            both = jnp.where(masks[k][j], far, near)
            xs[(k * ring + m) * 3 + j] = pltpu.roll(both, (dxs[k] + 1 - j + w) & (w - 1), 1)

    for k in range(frames):
        for y in range(h):
            unpack(k, y, y % PACK, hrecv[went_x[k], hslot[k] * tiles + y // PACK])
    for k in range(frames):
        for y in range(h):
            shift(k, y, red[k * h + y])

    def widen(t, edge):
        mid = sp[pl.ds(t * pb + ch, ch)]
        sp[pl.ds(t * pb, ch)] = jnp.where(lane_c == 0, edge, pltpu.roll(mid, 1, 1))
        sp[pl.ds(t * pb + 2 * ch, ch)] = jnp.where(lane_c == w - 1, edge, pltpu.roll(mid, w - 1, 1))

    def present(p):
        y = 2 * p
        rhs = jnp.concatenate([sp[pl.ds(y * pb, 3 * pb)], sp[pl.ds((y + 1) * pb, 3 * pb)]], axis=1)
        acc[p] = jnp.dot(wp[...], rhs, preferred_element_type=F32)

    for t in range(1, h + 1):
        widen(t, pltpu.roll(pk[...], (w - 2 * (t - 1)) % w, 1) if t > 1 else pk[...])
    for p in range(1, h // 2 - 1):
        present(p)
    arrive(pcopy)
    arrive(kcopy)
    widen(0, ends(krecv.at[0], 2 * h - 2, 2 * h))
    widen(h + 1, ends(krecv.at[1], 0, 2))
    present(0)
    present(h // 2 - 1)

    arrive(vcopy)
    arrive(ccopy)
    for k in range(frames):
        for m in range(reach):
            unpack(k, h + m, m % PACK, crecv[went_y[k], vslot[k] * ctiles + m // PACK])
    for k in range(frames):
        for m in range(reach):
            shift(k, h + m, vrecv[went_y[k], vslot[k] * reach + m])

    def window(y):
        rows = []
        for i in range(3):
            for k in range(frames):
                at = y + i - 1 - dys[k]
                at = jnp.where(at < 0, at + ring, at)
                part = xs[pl.ds((k * ring + at) * 3, 3)].reshape(depth, w)
                if y == 0 and i == 0:
                    part = jnp.where(r == 0, jnp.zeros_like(part), part)
                if y == h - 1 and i == 2:
                    part = jnp.where(r == nr - 1, jnp.zeros_like(part), part)
                rows.append(part)
        rows.append(rows[0][:lead])
        return jnp.concatenate(rows, axis=0)

    for p in range(h // 2):
        rhs = jnp.concatenate([window(2 * p), window(2 * p + 1)], axis=1)
        total = acc[p] + jnp.dot(ws[...], rhs, preferred_element_type=F32)
        total = jnp.maximum(total + bias, 0.0).astype(BF)
        out_ref[2 * p] = total[:, :w]
        out_ref[2 * p + 1] = total[:, w:]

    for copies in (hcopy, vcopy, qcopy, pcopy, ccopy, kcopy):
        finish(copies)


def place(rows_ref, out_ref):
    out_ref[...] = jnp.swapaxes(rows_ref[...], 0, 1)


def body(nr, nc, current_frame, history_frames, offsets, compress_weight, mixer_weight, mixer_bias):
    frames, ch, h, w = history_frames.shape
    cp = compress_weight.shape[0]
    depth = frames * cp
    reach = h // 2 + 1
    ring = h + reach
    tiles = -(-h // PACK)
    ctiles = -(-reach // PACK)
    mix = mixer_weight.transpose(0, 1, 3, 2)
    anyspace = pl.BlockSpec(memory_space=pl.ANY)
    vmem = pl.BlockSpec(memory_space=pltpu.VMEM)
    joined = pl.pallas_call(
        functools.partial(kernel, nr, nc),
        out_shape=pltpu.VMEM((h, ch, w), BF),
        in_specs=[pl.BlockSpec(memory_space=pltpu.SMEM), anyspace, anyspace, anyspace, vmem, vmem],
        out_specs=vmem,
        scratch_shapes=[
            pltpu.VMEM((frames, ch, h, w), BF),
            pltpu.VMEM((ch, h, w), BF),
            pltpu.VMEM(mix.shape, BF),
            pltpu.VMEM((frames * h, cp, w), BF),
            pltpu.VMEM((2, 2 * reach, cp, w), BF),
            pltpu.VMEM((2, 2 * reach, cp, w), BF),
            pltpu.VMEM((2, 2 * tiles, cp, w), BF),
            pltpu.VMEM((2, 2 * tiles, cp, w), BF),
            pltpu.VMEM((2, 2 * ctiles, cp, w), BF),
            pltpu.VMEM((2, 2 * ctiles, cp, w), BF),
            pltpu.VMEM((ch, w), BF),
            pltpu.VMEM((ch // 4, w), BF),
            pltpu.VMEM((2, ch // 4, w), BF),
            pltpu.VMEM((2, 2, ch // 4, w), BF),
            pltpu.VMEM((ch, w), BF),
            pltpu.VMEM(((h + 2) * 3 * ch, w), BF),
            pltpu.VMEM((frames * ring, cp, w), BF),
            pltpu.VMEM((frames * ring * 3, cp, w), BF),
            pltpu.VMEM((h // 2, ch, 2 * w), F32),
            pltpu.VMEM((ch, 9 * ch), BF),
            pltpu.VMEM((ch, -(-9 * depth // 128) * 128), BF),
            pltpu.SemaphoreType.DMA((frames + 2,)),
            pltpu.SemaphoreType.DMA((6, 2)),
            pltpu.SemaphoreType.DMA((6, 2)),
        ],
        compiler_params=pltpu.CompilerParams(collective_id=0, has_side_effects=True),
        name="join",
    )(offsets.T, history_frames, current_frame, mix, compress_weight, mixer_bias)
    return pl.pallas_call(
        place,
        out_shape=jax.ShapeDtypeStruct((ch, h, w), BF),
        in_specs=[vmem],
        out_specs=vmem,
        name="place",
    )(pltpu.with_memory_space_constraint(joined, pltpu.VMEM))


def solution(mesh):
    in_specs = (P(None, "rows", "cols"), P(None, None, "rows", "cols"), P(), P(), P(), P())
    out_specs = P(None, "rows", "cols")
    return jax.shard_map(
        functools.partial(body, mesh.shape["rows"], mesh.shape["cols"]),
        mesh=mesh, in_specs=in_specs, out_specs=out_specs, check_vma=False,
    )
```

time: 17.1 us -> 13.5 us (0.79)
  Pallas kernels: 16.9 us -> 13.4 us
    pallas_call x1, Pallas kernels: 16 us -> 12.4 us  [body(): pl.pallas_call(functools.partial(kernel, nr, nc), out_shape=pltpu.VMEM((h...]
where the time goes in v3:
time: 13.5 us; the launch traced here: 13.4 us
  Pallas kernels  13.4 us (99%)
    pallas_call x1, Pallas kernels, body(): pl.pallas_call(functools.partial(kernel, nr, nc), out_shape=pltpu.VMEM((h...  12.4 us
    pallas_call x1, Pallas kernels, body(): pl.pallas_call(place, out_shape=jax.ShapeDtypeStruct((ch, h, w), BF), in_...  0.93 us

profile of v3, /device:TPU:1, one launch (start us, length us, event | category | flops | bytes accessed | tf_op | source)
XLA Modules:
  0.0 13.4 jit_solution(1172321046068788100)
XLA Ops:
  0.0 12.4 %join.1.rows_ref = bf16[16,128,128]{2,1,0:T(8,128)(2,1)S(1)} custom-call(s32[2,3]{1,0:T(2,128)} %bitcast.3, bf16[3,128,16,128]{3,2,1,0:T(8,128)(2,1)} %hist_hbm.1, bf16[128,16,128]{2,1,0:T(8,128)(2,1)} %cur_hbm.1, bf16[3,3,224,128]{3,2,1,0:T(8,128)(2,1)} %bitcast.2, bf16[32,128]{1,0:T(8,128)(2,1)} %cw_ref.1, f32[128]{0:T(128)} %bias_ref.1), custom_call_target="tpu_custom_call" | custom-call | tf_op jit(solution)/shard_map/join/pallas_call | solution.py:333
  12.4 0.9 %place.1 = bf16[128,16,128]{2,1,0:T(8,128)(2,1)} custom-call(bf16[16,128,128]{2,1,0:T(8,128)(2,1)S(1)} %join.1.rows_ref), custom_call_target="tpu_custom_call" | custom-call | tf_op jit(solution)/shard_map/place/pallas_call | solution.py:367

commit v4 on v3

--- a/solution.py
+++ b/solution.py
@@ -28,46 +28,62 @@
 
 def kernel(
     nr, nc,
-    off, hist_hbm, cur_hbm, mix_hbm, cw_ref, bias_ref, out_ref,
-    hist, cur, mix, red, vsend, vrecv, hsend, hrecv, csend, crecv,
-    qfull, qsend, qrecv, krecv, pk, sp, unp, xs, acc, wp, ws, lsem, ssem, rsem,
+    off_hbm, hist_hbm, cur_hbm, mix_hbm, cw_hbm, bias_hbm, out_ref,
+    off, cw, bias_row, hist, cur, mix, red, vsend, vrecv, packs, hsend, hrecv, csend, crecv,
+    qfull, qsend, qrecv, krecv, pk, sp, unp, xs, acc, wp, ws, lsem, ssem, rsem, ready,
 ):
     frames, ch, h, w = hist.shape
-    cp = cw_ref.shape[0]
+    cp = cw.shape[0]
     depth = frames * cp
     reach = h // 2 + 1
     ring = h + reach
     pitch = w // PACK
     tiles = -(-h // PACK)
-    ctiles = -(-reach // PACK)
+    rest = reach - PACK
     pb = 3 * ch
     quarter = ch // 4
 
     r = lax.axis_index("rows")
     c = lax.axis_index("cols")
     has_up, has_dn, has_lf, has_rt = r > 0, r < nr - 1, c > 0, c < nc - 1
-    up_dev, dn_dev, lf_dev, rt_dev = (r - 1, c), (r + 1, c), (r, c - 1), (r, c + 1)
-
-    loads = [pltpu.make_async_copy(hist_hbm.at[k], hist.at[k], lsem.at[k]) for k in range(frames)]
-    load_cur = pltpu.make_async_copy(cur_hbm, cur, lsem.at[frames])
-    load_mix = pltpu.make_async_copy(mix_hbm, mix, lsem.at[frames + 1])
-    for x in (*loads, load_cur, load_mix):
+    above, below = (r - 1, has_up), (r + 1, has_dn)
+    before, after = (c - 1, has_lf), (c + 1, has_rt)
+
+    small = [
+        pltpu.make_async_copy(src, dst, lsem.at[n])
+        for n, (src, dst) in enumerate(((off_hbm, off), (cw_hbm, cw), (bias_hbm, bias_row)))
+    ]
+    loads = [pltpu.make_async_copy(hist_hbm.at[k], hist.at[k], lsem.at[3 + k]) for k in range(frames)]
+    load_cur = pltpu.make_async_copy(cur_hbm, cur, lsem.at[3 + frames])
+    load_mix = pltpu.make_async_copy(mix_hbm, mix, lsem.at[4 + frames])
+    for x in (*loads, *small, load_cur, load_mix):
         x.start()
 
     barrier = pltpu.get_barrier_semaphore()
-    for cond, dev in ((has_up, up_dev), (has_dn, dn_dev), (has_lf, lf_dev), (has_rt, rt_dev)):
+    near = ((r - 1, c, has_up), (r + 1, c, has_dn), (r, c - 1, has_lf), (r, c + 1, has_rt))
+    for rr, cc, cond in near:
         @pl.when(cond)
-        def _(dev=dev):
+        def _(dev=(rr, cc)):
             pl.semaphore_signal(barrier, inc=1, device_id=dev, device_id_type=MESH)
 
-    def remote(n, d, src, dst, sideways):
-        dev = ((rt_dev, lf_dev) if sideways else (dn_dev, up_dev))[d]
+    def number(*conds):
+        return sum(jnp.where(x, jnp.int32(1), jnp.int32(0)) for x in conds)
+
+    def remote(n, src, dst, dv=None, dh=None):
+        rr, sends, comes, m = r, True, True, 0
+        cc = c
+        if dv is not None:
+            (rr, sends), (_, comes) = (below, above) if dv == 0 else (above, below)
+            m = dv
+        if dh is not None:
+            (cc, out), (_, into) = (after, before) if dh == 0 else (before, after)
+            sends, comes = sends & out, comes & into
+            m = 2 * m + dh if dv is not None else dh
         copy = pltpu.make_async_remote_copy(
-            src_ref=src, dst_ref=dst, send_sem=ssem.at[n, d], recv_sem=rsem.at[n, d],
-            device_id=dev, device_id_type=MESH,
+            src_ref=src, dst_ref=dst, send_sem=ssem.at[n, m], recv_sem=rsem.at[n, m],
+            device_id=(rr, cc), device_id_type=MESH,
         )
-        ways = (has_rt, has_lf) if sideways else (has_dn, has_up)
-        return copy, ways[d], ways[1 - d]
+        return copy, sends, comes
 
     def start(copies):
         for copy, sends, _ in copies:
@@ -87,16 +103,19 @@
             def _(copy=copy):
                 copy.wait_send()
 
-    hcopy = [remote(0, d, hsend.at[d], hrecv.at[d], True) for d in (0, 1)]
-    vcopy = [remote(1, d, vsend.at[d], vrecv.at[d], False) for d in (0, 1)]
-    qcopy = [remote(2, d, qsend, qrecv.at[d], True) for d in (0, 1)]
+    hcopy = [remote(0, hsend.at[d], hrecv.at[d], dh=d) for d in (0, 1)]
+    vcopy = [remote(1, vsend.at[d], vrecv.at[d], dv=d) for d in (0, 1)]
+    qcopy = [remote(2, qsend, qrecv.at[d], dh=d) for d in (0, 1)]
     pcopy = [
-        remote(3, 0, sp.at[pl.ds(h * pb + ch, ch)], sp.at[pl.ds(ch, ch)], False),
-        remote(3, 1, sp.at[pl.ds(pb + ch, ch)], sp.at[pl.ds((h + 1) * pb + ch, ch)], False),
+        remote(3, sp.at[pl.ds(h * pb + ch, ch)], sp.at[pl.ds(ch, ch)], dv=0),
+        remote(3, sp.at[pl.ds(pb + ch, ch)], sp.at[pl.ds((h + 1) * pb + ch, ch)], dv=1),
     ]
-    ccopy = [remote(4, d, csend.at[d], crecv.at[d], False) for d in (0, 1)]
-    kcopy = [remote(5, d, qrecv, krecv.at[d], False) for d in (0, 1)]
-
+    corners = [(dv, dh) for dv in (0, 1) for dh in (0, 1)]
+    ccopy = [remote(4, csend.at[dv], crecv.at[dv, dh], dv, dh) for dv, dh in corners]
+    kcopy = [remote(5, qsend, krecv.at[dv, dh], dv, dh) for dv, dh in corners]
+
+    for x in small:
+        x.wait()
     dys = [off[0, k] for k in range(frames)]
     dxs = [off[1, k] for k in range(frames)]
     down, up = pick(dys, True), pick(dys, False)
@@ -126,49 +145,60 @@
 
     @pl.when(c == 0)
     def _():
-        clear(hrecv.at[0])
-        clear(qrecv.at[0])
+        for ref in (hrecv.at[0], qrecv.at[0], crecv.at[0, 0], crecv.at[1, 0], krecv.at[0, 0], krecv.at[1, 0]):
+            clear(ref)
 
     @pl.when(c == nc - 1)
     def _():
-        clear(hrecv.at[1])
-        clear(qrecv.at[1])
+        for ref in (hrecv.at[1], qrecv.at[1], crecv.at[0, 1], crecv.at[1, 1], krecv.at[0, 1], krecv.at[1, 1]):
+            clear(ref)
 
     for k in range(frames):
         loads[k].wait()
         rows = jnp.swapaxes(hist[k], 0, 1)
         for y in range(0, h, 2):
             rhs = jnp.concatenate([rows[y], rows[y + 1]], axis=1)
-            got = jnp.dot(cw_ref[...], rhs, preferred_element_type=F32).astype(BF)
+            got = jnp.dot(cw[...], rhs, preferred_element_type=F32).astype(BF)
             for e in (0, 1):
                 red[k * h + y + e] = got[:, e * w:(e + 1) * w]
 
-    lane = lax.broadcasted_iota(jnp.int32, (cp, w), 1)
-    for d in (0, 1):
-        for s in (0, 1):
-            frame, base = (right[s], REACH_X) if d == 0 else (left[s], 0)
-            for g in range(tiles):
-                tile = None
-                for q in range(min(PACK, h - PACK * g)):
-                    row = red[frame * h + PACK * g + q]
-                    turn = (base + pitch * q) % w
-                    row = pltpu.roll(row, turn, 1) if turn else row
-                    tile = row if tile is None else jnp.where(lane >= pitch * q, row, tile)
-                hsend[d, s * tiles + g] = tile
-
-    count = sum(jnp.where(x, jnp.int32(1), jnp.int32(0)) for x in (has_up, has_dn, has_lf, has_rt))
-    pl.semaphore_wait(barrier, count)
-    start(hcopy)
     for s in (0, 1):
         vsend[0, pl.ds(s * reach, reach)] = red[pl.ds(down[s] * h + h - reach, reach)]
         vsend[1, pl.ds(s * reach, reach)] = red[pl.ds(up[s] * h, reach)]
+    pl.semaphore_wait(barrier, number(has_up, has_dn, has_lf, has_rt))
+    for rr, cc, cond in near[:2]:
+        @pl.when(cond)
+        def _(dev=(rr, cc)):
+            pl.semaphore_signal(ready, inc=1, device_id=dev, device_id_type=MESH)
     start(vcopy)
+
+    lane = lax.broadcasted_iota(jnp.int32, (cp, w), 1)
+    for k in range(frames):
+        for g in range(tiles):
+            tile = None
+            for q in range(min(PACK, h - PACK * g)):
+                turn = jnp.where(dxs[k] > 0, jnp.int32((REACH_X + pitch * q) % w), jnp.int32(pitch * q))
+                row = pltpu.roll(red[k * h + PACK * g + q], turn, 1)
+                tile = row if tile is None else jnp.where(lane >= pitch * q, row, tile)
+            packs[k * tiles + g] = tile
+    for s in (0, 1):
+        for d in (0, 1):
+            frame = (right, left)[d][s]
+            hsend[d, pl.ds(s * tiles, tiles)] = packs[pl.ds(frame * tiles, tiles)]
+    start(hcopy)
+    for d in (0, 1):
+        at = [(down, up)[d][s] * tiles + (1 if d == 0 else 0) for s in (0, 1)]
+        for s in (0, 1):
+            csend[d, s] = packs[at[s]]
+        turned = pltpu.roll(packs[at[1] + 1], rest * pitch, 1)
+        csend[d, 2] = jnp.where(lane < rest * pitch, packs[at[0] + 1], turned)
+    pl.semaphore_wait(ready, number(has_up, has_dn))
+    start(ccopy)
 
     load_cur.wait()
     rows = jnp.swapaxes(cur[...], 0, 1)
     for y in range(h):
         sp[pl.ds((y + 1) * pb + ch, ch)] = rows[y]
-    start(pcopy)
     lane_c = lax.broadcasted_iota(jnp.int32, (ch, w), 1)
     tile = jnp.zeros((ch, w), BF)
     for y in range(h):
@@ -182,6 +212,8 @@
         small = jnp.where(lane_q >= 2 * h * g, turned, small)
     qsend[...] = small
     start(qcopy)
+    start(pcopy)
+    start(kcopy)
 
     load_mix.wait()
     for i in range(3):
@@ -195,22 +227,12 @@
     past = jnp.concatenate(past, axis=0)
     for n in range(0, ws.shape[1], ch):
         ws[:, n:n + ch] = jnp.swapaxes(past[n:n + ch], 0, 1)
-    wide = jnp.broadcast_to(bias_ref[...][None, :], (ch, ch))
+    wide = jnp.broadcast_to(bias_row[...][None, :], (ch, ch))
     eye = lax.broadcasted_iota(jnp.int32, (ch, ch), 0) == lax.broadcasted_iota(jnp.int32, (ch, ch), 1)
     bias = jnp.sum(jnp.where(eye, wide, 0.0), axis=1, keepdims=True)
 
     arrive(hcopy)
-    for s in (0, 1):
-        for d, frame in ((0, down[s]), (1, up[s])):
-            way, at = jnp.int32(0), jnp.int32(0)
-            for k in range(frames):
-                way = jnp.where(frame == k, went_x[k], way)
-                at = jnp.where(frame == k, hslot[k] * tiles, at)
-            first = at + (tiles - ctiles if d == 0 else 0)
-            csend[d, pl.ds(s * ctiles, ctiles)] = hrecv[way, pl.ds(first, ctiles)]
-    start(ccopy)
     arrive(qcopy)
-    start(kcopy)
 
     def ends(near, lf_turn, rt_turn):
         lf = jnp.concatenate(
@@ -273,18 +295,14 @@
         widen(t, pltpu.roll(pk[...], (w - 2 * (t - 1)) % w, 1) if t > 1 else pk[...])
     for p in range(1, h // 2 - 1):
         present(p)
-    arrive(pcopy)
-    arrive(kcopy)
-    widen(0, ends(krecv.at[0], 2 * h - 2, 2 * h))
-    widen(h + 1, ends(krecv.at[1], 0, 2))
-    present(0)
-    present(h // 2 - 1)
-
     arrive(vcopy)
     arrive(ccopy)
     for k in range(frames):
         for m in range(reach):
-            unpack(k, h + m, m % PACK, crecv[went_y[k], vslot[k] * ctiles + m // PACK])
+            at, q = vslot[k], jnp.int32(m)
+            if m >= PACK:
+                at, q = 2, rest * vslot[k] + (m - PACK)
+            unpack(k, h + m, q, crecv[went_y[k], went_x[k], at])
     for k in range(frames):
         for m in range(reach):
             shift(k, h + m, vrecv[went_y[k], vslot[k] * reach + m])
@@ -304,12 +322,22 @@
         rows.append(rows[0][:lead])
         return jnp.concatenate(rows, axis=0)
 
-    for p in range(h // 2):
+    def finish_pair(p):
         rhs = jnp.concatenate([window(2 * p), window(2 * p + 1)], axis=1)
         total = acc[p] + jnp.dot(ws[...], rhs, preferred_element_type=F32)
         total = jnp.maximum(total + bias, 0.0).astype(BF)
         out_ref[2 * p] = total[:, :w]
         out_ref[2 * p + 1] = total[:, w:]
+
+    for p in range(1, h // 2 - 1):
+        finish_pair(p)
+    arrive(pcopy)
+    arrive(kcopy)
+    widen(0, ends(krecv.at[0], 2 * h - 2, 2 * h))
+    widen(h + 1, ends(krecv.at[1], 0, 2))
+    for p in (0, h // 2 - 1):
+        present(p)
+        finish_pair(p)
 
     for copies in (hcopy, vcopy, qcopy, pcopy, ccopy, kcopy):
         finish(copies)
@@ -326,26 +354,29 @@
     reach = h // 2 + 1
     ring = h + reach
     tiles = -(-h // PACK)
-    ctiles = -(-reach // PACK)
     mix = mixer_weight.transpose(0, 1, 3, 2)
     anyspace = pl.BlockSpec(memory_space=pl.ANY)
     vmem = pl.BlockSpec(memory_space=pltpu.VMEM)
     joined = pl.pallas_call(
         functools.partial(kernel, nr, nc),
         out_shape=pltpu.VMEM((h, ch, w), BF),
-        in_specs=[pl.BlockSpec(memory_space=pltpu.SMEM), anyspace, anyspace, anyspace, vmem, vmem],
+        in_specs=[anyspace] * 6,
         out_specs=vmem,
         scratch_shapes=[
+            pltpu.SMEM((2, frames), jnp.int32),
+            pltpu.VMEM((cp, ch), BF),
+            pltpu.VMEM((ch,), F32),
             pltpu.VMEM((frames, ch, h, w), BF),
             pltpu.VMEM((ch, h, w), BF),
             pltpu.VMEM(mix.shape, BF),
             pltpu.VMEM((frames * h, cp, w), BF),
             pltpu.VMEM((2, 2 * reach, cp, w), BF),
             pltpu.VMEM((2, 2 * reach, cp, w), BF),
+            pltpu.VMEM((frames * tiles, cp, w), BF),
             pltpu.VMEM((2, 2 * tiles, cp, w), BF),
             pltpu.VMEM((2, 2 * tiles, cp, w), BF),
-            pltpu.VMEM((2, 2 * ctiles, cp, w), BF),
-            pltpu.VMEM((2, 2 * ctiles, cp, w), BF),
+            pltpu.VMEM((2, 3, cp, w), BF),
+            pltpu.VMEM((2, 2, 3, cp, w), BF),
             pltpu.VMEM((ch, w), BF),
             pltpu.VMEM((ch // 4, w), BF),
             pltpu.VMEM((2, ch // 4, w), BF),
@@ -357,9 +388,10 @@
             pltpu.VMEM((h // 2, ch, 2 * w), F32),
             pltpu.VMEM((ch, 9 * ch), BF),
             pltpu.VMEM((ch, -(-9 * depth // 128) * 128), BF),
-            pltpu.SemaphoreType.DMA((frames + 2,)),
-            pltpu.SemaphoreType.DMA((6, 2)),
-            pltpu.SemaphoreType.DMA((6, 2)),
+            pltpu.SemaphoreType.DMA((frames + 5,)),
+            pltpu.SemaphoreType.DMA((6, 4)),
+            pltpu.SemaphoreType.DMA((6, 4)),
+            pltpu.SemaphoreType.REGULAR,
         ],
         compiler_params=pltpu.CompilerParams(collective_id=0, has_side_effects=True),
         name="join",

time: 13.5 us -> 12.4 us (0.919)
  the two profiles are of different devices: /device:TPU:1 before, /device:TPU:17 now
where the time goes in v4:
time: 12.4 us; the launch traced here: 12.3 us
  Pallas kernels  12.3 us (99%)
    pallas_call x1, Pallas kernels, body(): pl.pallas_call(functools.partial(kernel, nr, nc), out_shape=pltpu.VMEM((h...  11.3 us
    pallas_call x1, Pallas kernels, body(): pl.pallas_call(place, out_shape=jax.ShapeDtypeStruct((ch, h, w), BF), in_...  0.93 us

profile of v4, /device:TPU:17, one launch (start us, length us, event | category | flops | bytes accessed | tf_op | source)
XLA Modules:
  0.0 12.3 jit_solution(9466224866460302906)
XLA Ops:
  0.0 11.3 %join.1.rows_ref = bf16[16,128,128]{2,1,0:T(8,128)(2,1)S(1)} custom-call(s32[2,3]{1,0:T(2,128)} %bitcast.3, bf16[3,128,16,128]{3,2,1,0:T(8,128)(2,1)} %hist_hbm.1, bf16[128,16,128]{2,1,0:T(8,128)(2,1)} %cur_hbm.1, bf16[3,3,224,128]{3,2,1,0:T(8,128)(2,1)} %bitcast.2, bf16[32,128]{1,0:T(8,128)(2,1)} %cw_hbm.1, f32[128]{0:T(128)} %bias_hbm.1), custom_call_target="tpu_custom_call" | custom-call | tf_op jit(solution)/shard_map/join/pallas_call | solution.py:360
  11.4 0.9 %place.1 = bf16[128,16,128]{2,1,0:T(8,128)(2,1)} custom-call(bf16[16,128,128]{2,1,0:T(8,128)(2,1)S(1)} %join.1.rows_ref), custom_call_target="tpu_custom_call" | custom-call | tf_op jit(solution)/shard_map/place/pallas_call | solution.py:399

commit v5 on v4

v5 whole, which is shorter than its diff:
```python
import functools

import jax
import jax.numpy as jnp
from jax import lax
from jax.experimental import pallas as pl
from jax.experimental.pallas import tpu as pltpu
from jax.sharding import PartitionSpec as P

MESH = pl.DeviceIdType.MESH
BF = jnp.bfloat16
F32 = jnp.float32
PACK = 7
CHUNKS = 4
REACH_X = 17


def pick(ds, positive):
    n = len(ds)
    first, last = jnp.int32(n - 1), jnp.int32(0)
    for k in range(n):
        hit = ds[k] > 0 if positive else ds[k] < 0
        last = jnp.where(hit, jnp.int32(k), last)
    for k in reversed(range(n)):
        hit = ds[k] > 0 if positive else ds[k] < 0
        first = jnp.where(hit, jnp.int32(k), first)
    return first, last


def kernel(
    nr, nc,
    off_hbm, hist_hbm, cur_hbm, mix_hbm, cw_hbm, bias_hbm, out_ref,
    off, cw, bias_row, hist, cur, mix, red, vsend, vrecv, packs, hsend, hrecv, csend, crecv_a, crecv_b,
    qfull, qsend, qrecv, krecv, pk, sp, unp, xs, acc, wp, ws, lsem, ssem, rsem, ready,
):
    frames, ch, h, w = hist.shape
    cp = cw.shape[0]
    depth = frames * cp
    reach = h // 2 + 1
    pitch = w // PACK
    tiles = -(-h // PACK)
    rest = reach - PACK
    own = frames * h
    pb = 3 * ch
    quarter = ch // 4

    r = lax.axis_index("rows")
    c = lax.axis_index("cols")
    has_up, has_dn, has_lf, has_rt = r > 0, r < nr - 1, c > 0, c < nc - 1
    above, below = (r - 1, has_up), (r + 1, has_dn)
    before, after = (c - 1, has_lf), (c + 1, has_rt)

    barrier = pltpu.get_barrier_semaphore()
    near = ((r - 1, c, has_up), (r + 1, c, has_dn), (r, c - 1, has_lf), (r, c + 1, has_rt))
    for rr, cc, cond in near:
        @pl.when(cond)
        def _(dev=(rr, cc)):
            pl.semaphore_signal(barrier, inc=1, device_id=dev, device_id_type=MESH)

    small = [
        pltpu.make_async_copy(src, dst, lsem.at[n])
        for n, (src, dst) in enumerate(((off_hbm, off), (cw_hbm, cw), (bias_hbm, bias_row)))
    ]
    loads = [pltpu.make_async_copy(hist_hbm.at[k], hist.at[k], lsem.at[3 + k]) for k in range(frames)]
    load_cur = pltpu.make_async_copy(cur_hbm, cur, lsem.at[3 + frames])
    load_mix = pltpu.make_async_copy(mix_hbm, mix, lsem.at[4 + frames])
    for x in (load_cur, *loads, *small, load_mix):
        x.start()

    def number(*conds):
        return sum(jnp.where(x, jnp.int32(1), jnp.int32(0)) for x in conds)

    def remote(n, src, dst, dv=None, dh=None):
        rr, sends, comes, m = r, True, True, 0
        cc = c
        if dv is not None:
            (rr, sends), (_, comes) = (below, above) if dv == 0 else (above, below)
            m = dv
        if dh is not None:
            (cc, out), (_, into) = (after, before) if dh == 0 else (before, after)
            sends, comes = sends & out, comes & into
            m = 2 * m + dh if dv is not None else dh
        copy = pltpu.make_async_remote_copy(
            src_ref=src, dst_ref=dst, send_sem=ssem.at[n, m], recv_sem=rsem.at[n, m],
            device_id=(rr, cc), device_id_type=MESH,
        )
        return copy, sends, comes

    def start(copies):
        for copy, sends, _ in copies:
            @pl.when(sends)
            def _(copy=copy):
                copy.start()

    def arrive(copies):
        for copy, _, comes in copies:
            @pl.when(comes)
            def _(copy=copy):
                copy.wait_recv()

    def finish(copies):
        for copy, sends, _ in copies:
            @pl.when(sends)
            def _(copy=copy):
                copy.wait_send()

    hcopy = [remote(0, hsend.at[d], hrecv.at[d], dh=d) for d in (0, 1)]
    def vpart(n, s):
        part = pl.ds(s * reach, reach)
        return [remote(n, vsend.at[d, part], vrecv.at[d, part], dv=d) for d in (0, 1)]

    vcopy, wcopy = vpart(1, 0), vpart(6, 1)
    qcopy = [remote(2, qsend, qrecv.at[d], dh=d) for d in (0, 1)]
    pcopy = [
        remote(3, sp.at[pl.ds(h * pb + ch, ch)], sp.at[pl.ds(ch, ch)], dv=0),
        remote(3, sp.at[pl.ds(pb + ch, ch)], sp.at[pl.ds((h + 1) * pb + ch, ch)], dv=1),
    ]
    crecv = (crecv_a, crecv_b)
    corners = [(dv, dh) for dv in (0, 1) for dh in (0, 1)]
    ccopy = [remote(4, csend.at[dv], crecv[dv].at[dh], dv, dh) for dv, dh in corners]
    kcopy = [remote(5, qsend, krecv.at[dv, dh], dv, dh) for dv, dh in corners]

    def clear(ref):
        ref[...] = jnp.zeros(ref.shape, BF)

    @pl.when(r == 0)
    def _():
        for ref in (xs.at[pl.ds(own * 3, 6 * reach)], krecv.at[0], sp.at[pl.ds(ch, ch)]):
            clear(ref)

    @pl.when(r == nr - 1)
    def _():
        for ref in (xs.at[pl.ds((own + 2 * reach) * 3, 6 * reach)], krecv.at[1], sp.at[pl.ds((h + 1) * pb + ch, ch)]):
            clear(ref)

    @pl.when(c == 0)
    def _():
        for ref in (hrecv.at[0], qrecv.at[0], crecv[0].at[0], crecv[1].at[0], krecv.at[0, 0], krecv.at[1, 0]):
            clear(ref)

    @pl.when(c == nc - 1)
    def _():
        for ref in (hrecv.at[1], qrecv.at[1], crecv[0].at[1], crecv[1].at[1], krecv.at[0, 1], krecv.at[1, 1]):
            clear(ref)

    for x in small:
        x.wait()
    dys = [off[0, k] for k in range(frames)]
    dxs = [off[1, k] for k in range(frames)]
    down, up = pick(dys, True), pick(dys, False)
    right, left = pick(dxs, True), pick(dxs, False)

    def slot(k, d, plus, minus):
        other = jnp.where(d > 0, plus[0], minus[0]) != k
        return jnp.where(other, jnp.int32(1), jnp.int32(0))

    vslot = [slot(k, dys[k], down, up) for k in range(frames)]
    hslot = [slot(k, dxs[k], right, left) for k in range(frames)]
    went_x = [jnp.where(dxs[k] > 0, jnp.int32(0), jnp.int32(1)) for k in range(frames)]
    went_y = [jnp.where(dys[k] > 0, jnp.int32(0), jnp.int32(1)) for k in range(frames)]

    load_cur.wait()
    rows = jnp.swapaxes(cur[...], 0, 1)
    for y in range(h):
        sp[pl.ds((y + 1) * pb + ch, ch)] = rows[y]
    lane_c = lax.broadcasted_iota(jnp.int32, (ch, w), 1)
    tile = jnp.zeros((ch, w), BF)
    for y in range(h):
        turned = pltpu.roll(rows[y], 2 * y + 1, 1)
        tile = jnp.where((lane_c == 2 * y) | (lane_c == 2 * y + 1), turned, tile)
    qfull[...] = tile
    small = qfull[pl.ds(0, quarter)]
    lane_q = lax.broadcasted_iota(jnp.int32, (quarter, w), 1)
    for g in range(1, 4):
        turned = pltpu.roll(qfull[pl.ds(g * quarter, quarter)], 2 * h * g, 1)
        small = jnp.where(lane_q >= 2 * h * g, turned, small)
    qsend[...] = small

    for k in range(frames):
        if k == 2:
            pl.semaphore_wait(barrier, number(has_up, has_dn, has_lf, has_rt))
            for rr, cc, cond in near[:2]:
                @pl.when(cond)
                def _(dev=(rr, cc)):
                    pl.semaphore_signal(ready, inc=1, device_id=dev, device_id_type=MESH)
            start(qcopy)
            start(pcopy)
        loads[k].wait()
        rows = jnp.swapaxes(hist[k], 0, 1)
        for y in range(0, h, 2):
            rhs = jnp.concatenate([rows[y], rows[y + 1]], axis=1)
            got = jnp.dot(cw[...], rhs, preferred_element_type=F32).astype(BF)
            for e in (0, 1):
                red[k * h + y + e] = got[:, e * w:(e + 1) * w]

    lane = lax.broadcasted_iota(jnp.int32, (cp, w), 1)
    for k in range(frames):
        for g in range(tiles):
            tile = None
            for q in range(min(PACK, h - PACK * g)):
                turn = jnp.where(dxs[k] > 0, jnp.int32((REACH_X + pitch * q) % w), jnp.int32(pitch * q))
                row = pltpu.roll(red[k * h + PACK * g + q], turn, 1)
                tile = row if tile is None else jnp.where(lane >= pitch * q, row, tile)
            packs[k * tiles + g] = tile
    for s in (0, 1):
        for d in (0, 1):
            frame = (right, left)[d][s]
            hsend[d, pl.ds(s * tiles, tiles)] = packs[pl.ds(frame * tiles, tiles)]
    start(hcopy)
    for s in (0, 1):
        vsend[0, pl.ds(s * reach, reach)] = red[pl.ds(down[s] * h + h - reach, reach)]
        vsend[1, pl.ds(s * reach, reach)] = red[pl.ds(up[s] * h, reach)]
    start(vcopy)

    for d in (0, 1):
        at = [(down, up)[d][s] * tiles + (1 if d == 0 else 0) for s in (0, 1)]
        for s in (0, 1):
            csend[d, s] = packs[at[s]]
        turned = pltpu.roll(packs[at[1] + 1], rest * pitch, 1)
        csend[d, 2] = jnp.where(lane < rest * pitch, packs[at[0] + 1], turned)
    pl.semaphore_wait(ready, number(has_up, has_dn))
    start(ccopy)
    start(kcopy)
    start(wcopy)

    load_mix.wait()
    for i in range(3):
        for j in range(3):
            wp[:, (3 * i + j) * ch:(3 * i + j + 1) * ch] = jnp.swapaxes(mix[i, j, :ch], 0, 1)
    past = [
        mix[i, j, ch + k * cp:ch + (k + 1) * cp] for i in range(3) for k in range(frames) for j in range(3)
    ]
    lead = ws.shape[1] - 9 * depth
    past.append(jnp.zeros((lead, ch), BF))
    past = jnp.concatenate(past, axis=0)
    for n in range(0, ws.shape[1], ch):
        ws[:, n:n + ch] = jnp.swapaxes(past[n:n + ch], 0, 1)
    wide = jnp.broadcast_to(bias_row[...][None, :], (ch, ch))
    eye = lax.broadcasted_iota(jnp.int32, (ch, ch), 0) == lax.broadcasted_iota(jnp.int32, (ch, ch), 1)
    bias = jnp.sum(jnp.where(eye, wide, 0.0), axis=1, keepdims=True)

    arrive(qcopy)

    def ends(near, lf_turn, rt_turn):
        lf = jnp.concatenate(
            [pltpu.roll(near[0], (2 * w - 2 * h * g - lf_turn) % w, 1) for g in range(4)], axis=0
        )
        rt = jnp.concatenate(
            [pltpu.roll(near[1], (2 * w - 2 * h * g - rt_turn) % w, 1) for g in range(4)], axis=0
        )
        return jnp.where((lane_c & 1) == 0, lf, rt)

    pk[...] = ends(qrecv, 0, 2)

    def shifter(dx):
        plus = dx > 0
        masks, kills = [], []
        for j in range(3):
            step = dx + 1 - j
            lo = jnp.where(plus, w - step, 0)
            hi = jnp.where(plus, w, -step)
            masks.append((lane >= lo) & (lane < hi))
            at = jnp.int32(-1)
            if j == 0:
                at = jnp.where(plus | (c > 0), at, -step)
            if j == 2:
                at = jnp.where(plus & (c == nc - 1), w - 1 - step, at)
            kills.append(lane == at)

        def unpack(at, q, tile):
            turn = (jnp.where(plus, w - REACH_X, 0) - pitch * q + w) & (w - 1)
            unp[at] = pltpu.roll(tile, turn, 1)

        def shift(at, row):
            far = unp[at]
            for j in range(3):
                near = row if j == 1 else jnp.where(kills[j], jnp.zeros_like(row), row)
                both = jnp.where(masks[j], far, near)
                xs[at * 3 + j] = pltpu.roll(both, (dx + 1 - j + w) & (w - 1), 1)

        return unpack, shift

    def halo(d):
        arrive([vcopy[d], wcopy[d], ccopy[2 * d], ccopy[2 * d + 1]])
        @pl.when((has_up, has_dn)[d])
        def _():
            for s in (0, 1):
                dx = off[1, (down, up)[d][s]]
                side = jnp.where(dx > 0, jnp.int32(0), jnp.int32(1))
                unpack, shift = shifter(dx)
                first = own + (2 * d + s) * reach
                for m in range(reach):
                    if m < PACK:
                        unpack(first + m, m, crecv[d][side, s])
                    else:
                        unpack(first + m, rest * s + m - PACK, crecv[d][side, 2])
                for m in range(reach):
                    shift(first + m, vrecv[d, s * reach + m])

    def widen(t, edge):
        mid = sp[pl.ds(t * pb + ch, ch)]
        sp[pl.ds(t * pb, ch)] = jnp.where(lane_c == 0, edge, pltpu.roll(mid, 1, 1))
        sp[pl.ds(t * pb + 2 * ch, ch)] = jnp.where(lane_c == w - 1, edge, pltpu.roll(mid, w - 1, 1))

    def present(p):
        y = 2 * p
        rhs = jnp.concatenate([sp[pl.ds(y * pb, 3 * pb)], sp[pl.ds((y + 1) * pb, 3 * pb)]], axis=1)
        acc[p] = jnp.dot(wp[...], rhs, preferred_element_type=F32)

    for t in range(1, h + 1):
        widen(t, pltpu.roll(pk[...], (w - 2 * (t - 1)) % w, 1) if t > 1 else pk[...])
    for p in range(1, h // 2 - 1):
        present(p)
    arrive(hcopy)
    for k in range(frames):
        unpack, shift = shifter(dxs[k])
        for y in range(h):
            unpack(k * h + y, y % PACK, hrecv[went_x[k], hslot[k] * tiles + y // PACK])
        for y in range(h):
            shift(k * h + y, red[k * h + y])

    def window(y):
        rows = []
        for i in range(3):
            for k in range(frames):
                at = y + i - 1 - dys[k]
                at = jnp.where(
                    at < 0, own + vslot[k] * reach + reach + at,
                    jnp.where(at >= h, own + (2 + vslot[k]) * reach + at - h, k * h + at),
                )
                part = xs[pl.ds(at * 3, 3)].reshape(depth, w)
                if y == 0 and i == 0:
                    part = jnp.where(r == 0, jnp.zeros_like(part), part)
                if y == h - 1 and i == 2:
                    part = jnp.where(r == nr - 1, jnp.zeros_like(part), part)
                rows.append(part)
        rows.append(rows[0][:lead])
        return jnp.concatenate(rows, axis=0)

    def finish_pair(p):
        rhs = jnp.concatenate([window(2 * p), window(2 * p + 1)], axis=1)
        total = acc[p] + jnp.dot(ws[...], rhs, preferred_element_type=F32)
        total = jnp.maximum(total + bias, 0.0).astype(BF)
        out_ref[2 * p] = total[:, :w]
        out_ref[2 * p + 1] = total[:, w:]

    last = h // 2 - 1
    free = (h - reach - 1) // 2

    def edge_pair(d):
        arrive([pcopy[d], kcopy[2 * d], kcopy[2 * d + 1]])
        if d == 0:
            widen(0, ends(krecv.at[0], 2 * h - 2, 2 * h))
        else:
            widen(h + 1, ends(krecv.at[1], 0, 2))
        present(last * d)
        finish_pair(last * d)

    first_above = (r % 2 == 1) | (r == 0)

    @pl.when(first_above)
    def _():
        halo(0)
        for p in range(1, free):
            finish_pair(p)
        edge_pair(0)
        halo(1)
        for p in range(free, last):
            finish_pair(p)
        edge_pair(1)

    @pl.when(jnp.logical_not(first_above))
    def _():
        halo(1)
        for p in range(last + 1 - free, last):
            finish_pair(p)
        edge_pair(1)
        halo(0)
        for p in range(1, last + 1 - free):
            finish_pair(p)
        edge_pair(0)

    for copies in (hcopy, vcopy, wcopy, qcopy, pcopy, ccopy, kcopy):
        finish(copies)


def place(rows_ref, out_hbm, turned, sem):
    n = out_hbm.shape[0] // CHUNKS
    copies = []
    for g in range(CHUNKS):
        part = pl.ds(g * n, n)
        turned[part] = jnp.swapaxes(rows_ref[:, part], 0, 1)
        copies.append(pltpu.make_async_copy(turned.at[part], out_hbm.at[part], sem.at[g]))
        copies[-1].start()
    for copy in copies:
        copy.wait()


def body(nr, nc, current_frame, history_frames, offsets, compress_weight, mixer_weight, mixer_bias):
    frames, ch, h, w = history_frames.shape
    cp = compress_weight.shape[0]
    depth = frames * cp
    reach = h // 2 + 1
    rows = frames * h + 4 * reach
    tiles = -(-h // PACK)
    mix = mixer_weight.transpose(0, 1, 3, 2)
    anyspace = pl.BlockSpec(memory_space=pl.ANY)
    vmem = pl.BlockSpec(memory_space=pltpu.VMEM)
    joined = pl.pallas_call(
        functools.partial(kernel, nr, nc),
        out_shape=pltpu.VMEM((h, ch, w), BF),
        in_specs=[anyspace] * 6,
        out_specs=vmem,
        scratch_shapes=[
            pltpu.SMEM((2, frames), jnp.int32),
            pltpu.VMEM((cp, ch), BF),
            pltpu.VMEM((ch,), F32),
            pltpu.VMEM((frames, ch, h, w), BF),
            pltpu.VMEM((ch, h, w), BF),
            pltpu.VMEM(mix.shape, BF),
            pltpu.VMEM((frames * h, cp, w), BF),
            pltpu.VMEM((2, 2 * reach, cp, w), BF),
            pltpu.VMEM((2, 2 * reach, cp, w), BF),
            pltpu.VMEM((frames * tiles, cp, w), BF),
            pltpu.VMEM((2, 2 * tiles, cp, w), BF),
            pltpu.VMEM((2, 2 * tiles, cp, w), BF),
            pltpu.VMEM((2, 3, cp, w), BF),
            pltpu.VMEM((2, 3, cp, w), BF),
            pltpu.VMEM((2, 3, cp, w), BF),
            pltpu.VMEM((ch, w), BF),
            pltpu.VMEM((ch // 4, w), BF),
            pltpu.VMEM((2, ch // 4, w), BF),
            pltpu.VMEM((2, 2, ch // 4, w), BF),
            pltpu.VMEM((ch, w), BF),
            pltpu.VMEM(((h + 2) * 3 * ch, w), BF),
            pltpu.VMEM((rows, cp, w), BF),
            pltpu.VMEM((rows * 3, cp, w), BF),
            pltpu.VMEM((h // 2, ch, 2 * w), F32),
            pltpu.VMEM((ch, 9 * ch), BF),
            pltpu.VMEM((ch, -(-9 * depth // 128) * 128), BF),
            pltpu.SemaphoreType.DMA((frames + 5,)),
            pltpu.SemaphoreType.DMA((7, 4)),
            pltpu.SemaphoreType.DMA((7, 4)),
            pltpu.SemaphoreType.REGULAR,
        ],
        compiler_params=pltpu.CompilerParams(collective_id=0, has_side_effects=True),
        name="join",
    )(offsets.T, history_frames, current_frame, mix, compress_weight, mixer_bias)
    return pl.pallas_call(
        place,
        out_shape=jax.ShapeDtypeStruct((ch, h, w), BF),
        in_specs=[vmem],
        out_specs=anyspace,
        scratch_shapes=[pltpu.VMEM((ch, h, w), BF), pltpu.SemaphoreType.DMA((CHUNKS,))],
        name="place",
    )(pltpu.with_memory_space_constraint(joined, pltpu.VMEM))


def solution(mesh):
    in_specs = (P(None, "rows", "cols"), P(None, None, "rows", "cols"), P(), P(), P(), P())
    out_specs = P(None, "rows", "cols")
    return jax.shard_map(
        functools.partial(body, mesh.shape["rows"], mesh.shape["cols"]),
        mesh=mesh, in_specs=in_specs, out_specs=out_specs, check_vma=False,
    )
```

time: 12.4 us -> 12.1 us (0.976)
  the two profiles are of different devices: /device:TPU:17 before, /device:TPU:0 now
where the time goes in v5:
time: 12.1 us; the launch traced here: 11.9 us
  Pallas kernels  11.9 us (98%)
    pallas_call x1, Pallas kernels, body(): pl.pallas_call(functools.partial(kernel, nr, nc), out_shape=pltpu.VMEM((h...  11.1 us
    pallas_call x1, Pallas kernels, body(): pl.pallas_call(place, out_shape=jax.ShapeDtypeStruct((ch, h, w), BF), in_...  0.87 us

profile of v5, /device:TPU:0, one launch (start us, length us, event | category | flops | bytes accessed | tf_op | source)
XLA Modules:
  0.0 11.9 jit_solution(13223970282452516297)
XLA Ops:
  0.0 11.1 %join.1.rows_ref = bf16[16,128,128]{2,1,0:T(8,128)(2,1)S(1)} custom-call(s32[2,3]{1,0:T(2,128)} %bitcast.3, bf16[3,128,16,128]{3,2,1,0:T(8,128)(2,1)} %hist_hbm.1, bf16[128,16,128]{2,1,0:T(8,128)(2,1)} %cur_hbm.1, bf16[3,3,224,128]{3,2,1,0:T(8,128)(2,1)} %bitcast.2, bf16[32,128]{1,0:T(8,128)(2,1)} %cw_hbm.1, f32[128]{0:T(128)} %bias_hbm.1), custom_call_target="tpu_custom_call" | custom-call | tf_op jit(solution)/shard_map/join/pallas_call | solution.py:409
  11.1 0.9 %place.1 = bf16[128,16,128]{2,1,0:T(8,128)(2,1)} custom-call(bf16[16,128,128]{2,1,0:T(8,128)(2,1)S(1)} %join.1.rows_ref), custom_call_target="tpu_custom_call" | custom-call | tf_op jit(solution)/shard_map/place/pallas_call | solution.py:449

commit v6 on v5

--- a/solution.py
+++ b/solution.py
@@ -239,6 +239,24 @@
     eye = lax.broadcasted_iota(jnp.int32, (ch, ch), 0) == lax.broadcasted_iota(jnp.int32, (ch, ch), 1)
     bias = jnp.sum(jnp.where(eye, wide, 0.0), axis=1, keepdims=True)
 
+    filled = []
+    for k in range(frames):
+        mine = []
+        for j in range(3):
+            step = dxs[k] + 1 - j
+            lo = jnp.where(dxs[k] > 0, 0, w + step)
+            hi = jnp.where(dxs[k] > 0, step, w)
+            mine.append((lane >= lo) & (lane < hi))
+        filled.append(mine)
+        for y in range(h):
+            row = red[k * h + y]
+            for j in range(3):
+                moved = pltpu.roll(row, (dxs[k] + 1 - j + w) & (w - 1), 1)
+                if j != 1:
+                    out = (lane == 0) & (c == 0) if j == 0 else (lane == w - 1) & (c == nc - 1)
+                    moved = jnp.where(out, jnp.zeros_like(moved), moved)
+                xs[(k * h + y) * 3 + j] = moved
+
     arrive(qcopy)
 
     def ends(near, lf_turn, rt_turn):
@@ -313,11 +331,13 @@
         present(p)
     arrive(hcopy)
     for k in range(frames):
-        unpack, shift = shifter(dxs[k])
+        base = -jnp.where(dxs[k] > 0, REACH_X, 0) + 2 * w
         for y in range(h):
-            unpack(k * h + y, y % PACK, hrecv[went_x[k], hslot[k] * tiles + y // PACK])
-        for y in range(h):
-            shift(k * h + y, red[k * h + y])
+            tile = hrecv[went_x[k], hslot[k] * tiles + y // PACK]
+            for j in range(3):
+                turn = (dxs[k] + 1 - j - pitch * (y % PACK) + base) & (w - 1)
+                at = (k * h + y) * 3 + j
+                xs[at] = jnp.where(filled[k][j], pltpu.roll(tile, turn, 1), xs[at])
 
     def window(y):
         rows = []

time: 12.1 us -> 11.9 us (0.983)
  the two profiles are of different devices: /device:TPU:0 before, /device:TPU:1 now
where the time goes in v6:
time: 11.9 us; the launch traced here: 11.7 us
  Pallas kernels  11.7 us (98%)
    pallas_call x1, Pallas kernels, body(): pl.pallas_call(functools.partial(kernel, nr, nc), out_shape=pltpu.VMEM((h...  10.9 us
    pallas_call x1, Pallas kernels, body(): pl.pallas_call(place, out_shape=jax.ShapeDtypeStruct((ch, h, w), BF), in_...  0.87 us

profile of v6, /device:TPU:1, one launch (start us, length us, event | category | flops | bytes accessed | tf_op | source)
XLA Modules:
  0.0 11.7 jit_solution(14480249029370188475)
XLA Ops:
  0.0 10.9 %join.1.rows_ref = bf16[16,128,128]{2,1,0:T(8,128)(2,1)S(1)} custom-call(s32[2,3]{1,0:T(2,128)} %bitcast.3, bf16[3,128,16,128]{3,2,1,0:T(8,128)(2,1)} %hist_hbm.1, bf16[128,16,128]{2,1,0:T(8,128)(2,1)} %cur_hbm.1, bf16[3,3,224,128]{3,2,1,0:T(8,128)(2,1)} %bitcast.2, bf16[32,128]{1,0:T(8,128)(2,1)} %cw_hbm.1, f32[128]{0:T(128)} %bias_hbm.1), custom_call_target="tpu_custom_call" | custom-call | tf_op jit(solution)/shard_map/join/pallas_call | solution.py:429
  10.9 0.9 %place.1 = bf16[128,16,128]{2,1,0:T(8,128)(2,1)} custom-call(bf16[16,128,128]{2,1,0:T(8,128)(2,1)S(1)} %join.1.rows_ref), custom_call_target="tpu_custom_call" | custom-call | tf_op jit(solution)/shard_map/place/pallas_call | solution.py:469

commit v7 on v6

--- a/solution.py
+++ b/solution.py
@@ -193,6 +193,13 @@
             for e in (0, 1):
                 red[k * h + y + e] = got[:, e * w:(e + 1) * w]
 
+    @pl.when(r > 0)
+    def _():
+        for s in (0, 1):
+            vsend[0, pl.ds(s * reach, reach)] = red[pl.ds(down[s] * h + h - reach, reach)]
+            vsend[1, pl.ds(s * reach, reach)] = red[pl.ds(up[s] * h, reach)]
+        start(vcopy)
+
     lane = lax.broadcasted_iota(jnp.int32, (cp, w), 1)
     for k in range(frames):
         for g in range(tiles):
@@ -207,10 +214,14 @@
             frame = (right, left)[d][s]
             hsend[d, pl.ds(s * tiles, tiles)] = packs[pl.ds(frame * tiles, tiles)]
     start(hcopy)
-    for s in (0, 1):
-        vsend[0, pl.ds(s * reach, reach)] = red[pl.ds(down[s] * h + h - reach, reach)]
-        vsend[1, pl.ds(s * reach, reach)] = red[pl.ds(up[s] * h, reach)]
-    start(vcopy)
+
+    @pl.when(r == 0)
+    def _():
+        for s in (0, 1):
+            vsend[0, pl.ds(s * reach, reach)] = red[pl.ds(down[s] * h + h - reach, reach)]
+            vsend[1, pl.ds(s * reach, reach)] = red[pl.ds(up[s] * h, reach)]
+        start(vcopy)
+
 
     for d in (0, 1):
         at = [(down, up)[d][s] * tiles + (1 if d == 0 else 0) for s in (0, 1)]

time: 11.9 us -> 12 us (level)
  the two profiles are of different devices: /device:TPU:1 before, /device:TPU:0 now
where the time goes in v7:
time: 12 us; the launch traced here: 11.9 us
  Pallas kernels  11.8 us (98%)
    pallas_call x1, Pallas kernels, body(): pl.pallas_call(functools.partial(kernel, nr, nc), out_shape=pltpu.VMEM((h...  11 us
    pallas_call x1, Pallas kernels, body(): pl.pallas_call(place, out_shape=jax.ShapeDtypeStruct((ch, h, w), BF), in_...  0.87 us

profile of v7, /device:TPU:0, one launch (start us, length us, event | category | flops | bytes accessed | tf_op | source)
XLA Modules:
  0.0 11.9 jit_solution(18017177943727908586)
XLA Ops:
  0.0 11.0 %join.1.rows_ref = bf16[16,128,128]{2,1,0:T(8,128)(2,1)S(1)} custom-call(s32[2,3]{1,0:T(2,128)} %bitcast.3, bf16[3,128,16,128]{3,2,1,0:T(8,128)(2,1)} %hist_hbm.1, bf16[128,16,128]{2,1,0:T(8,128)(2,1)} %cur_hbm.1, bf16[3,3,224,128]{3,2,1,0:T(8,128)(2,1)} %bitcast.2, bf16[32,128]{1,0:T(8,128)(2,1)} %cw_hbm.1, f32[128]{0:T(128)} %bias_hbm.1), custom_call_target="tpu_custom_call" | custom-call | tf_op jit(solution)/shard_map/join/pallas_call | solution.py:440
  11.0 0.9 %place.1 = bf16[128,16,128]{2,1,0:T(8,128)(2,1)} custom-call(bf16[16,128,128]{2,1,0:T(8,128)(2,1)S(1)} %join.1.rows_ref), custom_call_target="tpu_custom_call" | custom-call | tf_op jit(solution)/shard_map/place/pallas_call | solution.py:480
